TPU v7x, 32 devices: a whole 2x2x4 slice. The times are simulated.
32 devices in a mesh: frames: 8 (over z, x), heads: 4 (over y, core).
Axes of the slice: x: 2, y: 2, z: 4, core: 2. Of those that a mesh axis runs over, the one named last changes fastest.
Arguments:
- queries: bfloat16 [8192, 2560], P('frames', 'heads'), may hold values from -6 to 6, as said below
- keys: bfloat16 [8192, 2560], P('frames', 'heads'), may hold values from -6 to 6, as said below
- values: bfloat16 [8192, 2560], P('frames', 'heads'), may hold values from -6 to 6
- block_ids: int32 [64, 4], replicated, may hold values from 0 to 63, as said below
- counts: int32 [64], P('frames'), may hold values from 1 to 4
- w_out: bfloat16 [2560, 5120], P('heads'), may hold values from -0.125 to 0.125
Outputs:
- projected: bfloat16 [8192, 5120], P('frames', 'heads')
Inputs may be any that keep to these rules, and one draw needn't show every extreme that they name: `block_ids`: block j is held by index j // 8 of frames. Counted with repeats, the entries of the 8 query blocks of one index of frames name at most 4 blocks held by any one index, and exactly 4 held by some index. Entries of a row may repeat. `queries`: drawn in float32 and rounded once. `keys`: drawn in float32 and rounded once.
All inputs are finite; a program needn't handle non-finite values.
Results may differ from a plain program's by a relative error of at most 0.0052.
Values may be sent and summed in bfloat16 or wider, within the bound.
A program may use at most 192 MiB of HBM per device.

v0:
```python
import functools
import math

import jax
import jax.numpy as jnp
from jax import lax
from jax.experimental import pallas as pl
from jax.experimental.pallas import tpu as pltpu
from jax.sharding import PartitionSpec as P

DH = 128
TILE = 128
MESH = pl.DeviceIdType.MESH
F32 = jnp.float32
PAIR = 2
PARTS = 2
UNROLL = 2
AHEAD = 2
VMEM_BYTES = 67043328
NT_DIMS = (((1,), (1,)), ((), ()))


def head_columns(h):
    return slice(h * DH, (h + 1) * DH)


class direct_exchange:
    def __init__(self, dims, pick_ref, k_ref, v_ref, recv, send, kv_send, kv_recv):
        self.frames, _, _, _, self.capacity, self.heads, self.slots = dims
        self.pick_ref, self.k_ref, self.v_ref, self.recv = pick_ref, k_ref, v_ref, recv
        self.send, self.kv_send, self.kv_recv = send, kv_send, kv_recv
        self.me_f, self.me_p = lax.axis_index("frames"), lax.axis_index("heads")

    def copy(self, h, target, origin):
        return pltpu.make_async_remote_copy(
            src_ref=self.send.at[h % self.slots, target],
            dst_ref=self.recv[h].at[pl.ds(origin * self.capacity, self.capacity)],
            send_sem=self.kv_send.at[h, target],
            recv_sem=self.kv_recv.at[h, origin],
            device_id=(target, self.me_p),
            device_id_type=MESH,
        )

    def others(self, action):
        @pl.loop(1, self.frames)
        def _(step):
            action(lax.rem(self.me_f + step, self.frames))

    def pick(self, target, c):
        return self.pick_ref[(target * self.frames + self.me_f) * self.capacity + c]

    def build(self, h):
        if h >= self.slots:
            self.others(lambda target: self.copy(h - self.slots, target, self.me_f).wait_send())

        def fill(target):
            for c in range(self.capacity):
                index = self.pick(target, c)
                self.send[h % self.slots, target, c, 0] = self.k_ref[index, :, head_columns(h)]
                self.send[h % self.slots, target, c, 1] = self.v_ref[index, :, head_columns(h)]

        self.others(fill)
        for c in range(self.capacity):
            index = self.pick(self.me_f, c)
            self.recv[h][self.me_f * self.capacity + c, 0] = self.k_ref[index, :, head_columns(h)]
            self.recv[h][self.me_f * self.capacity + c, 1] = self.v_ref[index, :, head_columns(h)]

    def start(self, h):
        self.others(lambda target: self.copy(h, target, self.me_f).start())

    def prepare(self):
        self.build(0)

    def begin(self):
        self.start(0)

    def follow(self):
        if self.heads > 1:
            self.build(1)
            self.start(1)

    def receive(self, h, midway):
        if h + 2 < self.heads:
            self.build(h + 2)
        midway()
        self.others(lambda origin: self.copy(h, origin, origin).wait_recv())
        if h + 2 < self.heads:
            self.start(h + 2)

    def drain(self):
        for h in range(max(0, self.heads - self.slots), self.heads):
            self.others(lambda target: self.copy(h, target, self.me_f).wait_send())


class relay_exchange:
    def __init__(
        self, dims, pick_ref, k_ref, v_ref, recv,
        picked, up_send, up_recv, down_send, down_recv, x_send, x_recv, *passing,
    ):
        self.frames, _, self.blocks, _, self.capacity, self.heads, _ = dims
        self.line = self.frames // PAIR
        self.pick_ref, self.k_ref, self.v_ref, self.recv = pick_ref, k_ref, v_ref, recv
        self.picked, self.x_send, self.x_recv = picked, x_send, x_recv
        self.sems = ((up_send, up_recv), (down_send, down_recv))
        self.passing = passing
        self.me_f, self.me_p = lax.axis_index("frames"), lax.axis_index("heads")
        self.z, self.x = self.me_f // PAIR, self.me_f % PAIR
        self.partner = self.z * PAIR + (PAIR - 1 - self.x)

    def held(self, h, way, far):
        return self.passing[(h * 2 + way) * (self.line - 1) + far - 1]

    def at(self, way, steps):
        return self.z + steps if way == 0 else self.z - steps

    def inside(self, position):
        return (position >= 0) & (position < self.line)

    def onward(self, h, way, far, kv):
        source = (self.k_ref, self.v_ref)[kv].at[:, :, head_columns(h)]
        if far > 0:
            source = self.held(h, way, far).at[kv]
        send_sem, recv_sem = self.sems[way]
        return pltpu.make_async_remote_copy(
            src_ref=source,
            dst_ref=self.held(h, way, far + 1).at[kv],
            send_sem=send_sem.at[h, far, kv],
            recv_sem=recv_sem.at[h, far, kv],
            device_id=(self.at(way, 1) * PAIR + self.x, self.me_p),
            device_id_type=MESH,
        )

    def beside(self, h, origin_z, column):
        return pltpu.make_async_remote_copy(
            src_ref=self.picked.at[h, origin_z],
            dst_ref=self.recv[h].at[
                pl.ds((origin_z * PAIR + column) * self.capacity, self.capacity)
            ],
            send_sem=self.x_send.at[h, origin_z],
            recv_sem=self.x_recv.at[h, origin_z],
            device_id=(self.partner, self.me_p),
            device_id_type=MESH,
        )

    def send_on(self, h, way, far):
        @pl.when(self.inside(self.at(way, 1)))
        def _():
            for kv in range(2):
                self.onward(h, way, far, kv).start()

    def hand_out(self, h, origin_z, load):
        origin = origin_z * PAIR + self.x
        for c in range(self.capacity):
            theirs = self.pick_ref[(self.partner * self.frames + origin) * self.capacity + c]
            for kv in range(2):
                self.picked[h, origin_z, c, kv] = load(kv, theirs)
        for c in range(self.capacity):
            ours = self.pick_ref[(self.me_f * self.frames + origin) * self.capacity + c]
            for kv in range(2):
                self.recv[h][origin * self.capacity + c, kv] = load(kv, ours)
        self.beside(h, origin_z, self.x).start()

    def own(self, h):
        def load(kv, index):
            return (self.k_ref, self.v_ref)[kv][index, :, head_columns(h)]

        self.hand_out(h, self.z, load)

    def arrive(self, h, far):
        for way in range(2):
            @pl.when(self.inside(self.at(way, -far)))
            def _():
                for kv in range(2):
                    self.onward(h, way, far - 1, kv).wait_recv()
                if far + 1 < self.line:
                    self.send_on(h, way, far)

        for way in range(2):
            @pl.when(self.inside(self.at(way, -far)))
            def _():
                held = self.held(h, way, far)
                self.hand_out(h, self.at(way, -far), lambda kv, index: held[kv, index])

    def prepare(self):
        pass

    def begin(self):
        for h in range(min(AHEAD, self.heads)):
            for way in range(2):
                self.send_on(h, way, 0)

    def follow(self):
        self.own(0)

    def receive(self, h, midway):
        for far in range(1, self.line):
            if far == self.line - 1:
                midway()
            self.arrive(h, far)
            if far == 1 and h + AHEAD < self.heads:
                for way in range(2):
                    self.send_on(h + AHEAD, way, 0)
        if h + 1 < self.heads:
            self.own(h + 1)

        @pl.loop(0, self.line)
        def _(origin_z):
            self.beside(h, origin_z, PAIR - 1 - self.x).wait_recv()

    def drain(self):
        for h in range(self.heads):
            for way in range(2):
                for far in range(self.line - 1):
                    @pl.when(self.inside(self.at(way, -far)) & self.inside(self.at(way, 1)))
                    def _():
                        for kv in range(2):
                            self.onward(h, way, far, kv).wait_send()

            @pl.loop(0, self.line)
            def _(origin_z):
                self.beside(h, origin_z, self.x).wait_send()


def layer_kernel(
    dims, relayed, pick_ref, slot_ref, count_ref, q_ref, k_ref, v_ref, w_ref, out_ref,
    rows, attn, acc, w_send, w_recv, a_send, a_recv, own_sem, *kv_refs,
):
    frames, peers, blocks, select, capacity, heads, slots = dims
    recv, kv_refs = kv_refs[:heads], kv_refs[heads:]
    me_f, me_p = lax.axis_index("frames"), lax.axis_index("heads")
    depth = heads * DH
    features = rows.shape[2]

    barrier = pltpu.get_barrier_semaphore()

    @pl.loop(1, frames)
    def _(step):
        pl.semaphore_signal(
            barrier, inc=1, device_id=(lax.rem(me_f + step, frames), me_p), device_id_type=MESH
        )

    @pl.loop(1, peers)
    def _(step):
        pl.semaphore_signal(
            barrier, inc=1, device_id=(me_f, lax.rem(me_p + step, peers)), device_id_type=MESH
        )

    def columns_of(peer):
        return pl.ds(pl.multiple_of(peer * features, features), features)

    own_rows = pltpu.make_async_copy(w_ref.at[:, columns_of(me_p)], rows.at[me_p], own_sem)
    own_rows.start()

    exchange = (relay_exchange if relayed else direct_exchange)(
        dims, pick_ref, k_ref, v_ref, recv, *kv_refs
    )

    def w_copy(target, origin):
        return pltpu.make_async_remote_copy(
            src_ref=w_ref.at[:, columns_of(target)],
            dst_ref=rows.at[origin],
            send_sem=w_send.at[target],
            recv_sem=w_recv.at[origin],
            device_id=(me_f, target),
            device_id_type=MESH,
        )

    part_blocks = blocks // PARTS
    part_rows = part_blocks * TILE

    def a_copy(h, part, target, origin):
        held = attn.at[h, origin, pl.ds(part * part_rows, part_rows)]
        return pltpu.make_async_remote_copy(
            src_ref=held,
            dst_ref=held,
            send_sem=a_send.at[h, part, target, origin],
            recv_sem=a_recv.at[h, part, origin],
            device_id=(me_f, target),
            device_id_type=MESH,
        )

    twin = me_p + 1 - 2 * lax.rem(me_p, 2)

    def over_alike(action):
        @pl.loop(1, peers // 2)
        def _(step):
            action(lax.rem(me_p + 2 * step, peers))

    def over_twins(action):
        @pl.loop(0, peers // 2)
        def _(step):
            action(lax.rem(twin + 2 * step, peers))

    def share(h, part):
        over_alike(lambda target: a_copy(h, part, target, me_p).start())
        a_copy(h, part, twin, me_p).start()

    def finish(h):
        if h == 0:
            own_rows.wait()
            over_peers(lambda origin: w_copy(origin, origin).wait_recv())
        for part in range(PARTS):

            def relay(origin):
                a_copy(h, part, origin, origin).wait_recv()
                a_copy(h, part, twin, origin).start()

            over_alike(relay)
        for part in range(PARTS):
            over_twins(lambda origin: a_copy(h, part, origin, origin).wait_recv())
            project(h, part)

    def drain_attn(h, part):
        over_alike(lambda target: a_copy(h, part, target, me_p).wait_send())
        a_copy(h, part, twin, me_p).wait_send()
        over_alike(lambda origin: a_copy(h, part, twin, origin).wait_send())

    def over_peers(action):
        @pl.loop(1, peers)
        def _(step):
            action(lax.rem(me_p + step, peers))

    def attend(h, part):
        @pl.loop(part * part_blocks, (part + 1) * part_blocks, unroll=UNROLL)
        def _(b):
            q = q_ref[b, :, head_columns(h)]
            picks = [slot_ref[b * select + s] for s in range(select)]
            keyset = jnp.concatenate(
                [k_ref[b, :, head_columns(h)]] + [recv[h][i, 0] for i in picks], axis=0
            )
            valueset = jnp.concatenate(
                [v_ref[b, :, head_columns(h)]] + [recv[h][i, 1] for i in picks], axis=0
            )
            scores = lax.dot_general(q, keyset, NT_DIMS, preferred_element_type=F32)
            scores = scores * (1.0 / DH**0.5)
            position = lax.broadcasted_iota(jnp.int32, scores.shape, 1)
            scores = jnp.where(position < (count_ref[b] + 1) * TILE, scores, -jnp.inf)
            top = jnp.max(scores, axis=1, keepdims=True)
            probs = jnp.exp(scores - top)
            denom = jnp.sum(probs, axis=1, keepdims=True)
            mixed = jnp.dot(probs.astype(jnp.bfloat16), valueset, preferred_element_type=F32)
            attn[h, me_p, pl.ds(pl.multiple_of(b * TILE, TILE), TILE), :] = (mixed / denom).astype(
                jnp.bfloat16
            )

    row_tile = 2 * TILE

    def project(h, part):
        @pl.loop(part * part_rows // row_tile, (part + 1) * part_rows // row_tile)
        def _(r):
            span = pl.ds(pl.multiple_of(r * row_tile, row_tile), row_tile)
            left = jnp.concatenate([attn[h, p, span, :] for p in range(peers)], axis=1)
            right = jnp.concatenate([rows[p, head_columns(h), :] for p in range(peers)], axis=0)
            term = jnp.dot(left, right, preferred_element_type=F32)
            if h > 0:
                term = term + acc[span, :]
            if h == heads - 1:
                out_ref[span, :] = term.astype(out_ref.dtype)
            else:
                acc[span, :] = term

    exchange.prepare()
    pl.semaphore_wait(barrier, frames + peers - 2)
    exchange.begin()
    over_peers(lambda target: w_copy(target, me_p).start())
    exchange.follow()
    for h in range(heads):
        exchange.receive(h, (lambda: finish(h - 1)) if h > 0 else (lambda: None))
        for part in range(PARTS):
            attend(h, part)
            share(h, part)
    finish(heads - 1)
    exchange.drain()
    over_peers(lambda target: w_copy(target, me_p).wait_send())
    for h in range(heads):
        for part in range(PARTS):
            drain_attn(h, part)


def shards(queries, keys, values, block_ids, counts, w_out):
    frames = lax.axis_size("frames")
    peers = lax.axis_size("heads")
    here = lax.axis_index("frames")
    tokens, width = queries.shape
    blocks = tokens // TILE
    select = block_ids.shape[1]
    heads = width // DH
    requests = blocks * select
    capacity = max(2, (requests + frames - 1) // frames)
    features = w_out.shape[1] // peers
    slots = min(3, heads)

    ids = block_ids.reshape(frames, requests)
    owner = ids // blocks
    order = jnp.arange(requests, dtype=jnp.int32)
    same = (owner[:, :, None] == owner[:, None, :]) & (order[:, None] < order[None, :])
    slot = owner * capacity + jnp.sum(same.astype(jnp.int32), axis=1)
    hit = slot[:, None, :] == jnp.arange(frames * capacity, dtype=jnp.int32)[:, None]
    pick = jnp.sum(jnp.where(hit, (ids % blocks)[:, None, :], 0), axis=2).reshape(-1)
    my_slot = lax.dynamic_slice_in_dim(slot, here, 1, 0).reshape(requests)

    smem = pl.BlockSpec(memory_space=pltpu.SMEM)
    vmem = pl.BlockSpec(memory_space=pltpu.VMEM)
    tiles = (blocks, TILE, width)
    dma = pltpu.SemaphoreType.DMA
    bf16 = jnp.bfloat16
    line = frames // PAIR
    common = [
        pltpu.VMEM((peers, width, features), bf16),
        pltpu.VMEM((heads, peers, tokens, DH), bf16),
        pltpu.VMEM((tokens, features), F32),
    ]
    common_sems = [
        dma((peers,)), dma((peers,)), dma((heads, PARTS, peers, peers)),
        dma((heads, PARTS, peers)), dma,
    ]
    recv = [pltpu.VMEM((frames * capacity, 2, TILE, DH), bf16)] * heads
    picked = pltpu.VMEM((heads, line, capacity, 2, TILE, DH), bf16)
    passing = [pltpu.VMEM((2, blocks, TILE, DH), bf16)] * (heads * 2 * (line - 1))
    operands = tokens * (3 * width + features) * 2
    needed = operands + sum(
        math.prod(m.shape) * jnp.dtype(m.dtype).itemsize
        for m in common + recv + [picked] + passing
    )
    relayed = frames % PAIR == 0 and needed < VMEM_BYTES * 15 // 16
    if relayed:
        extra = [picked] + [dma((heads, line, 2))] * 4 + [dma((heads, line))] * 2 + passing
    else:
        extra = [
            pltpu.VMEM((slots, frames, capacity, 2, TILE, DH), bf16),
            dma((heads, frames)),
            dma((heads, frames)),
        ]
    dims = (frames, peers, blocks, select, capacity, heads, slots)
    return pl.pallas_call(
        functools.partial(layer_kernel, dims, relayed),
        out_shape=jax.ShapeDtypeStruct((tokens, features), bf16),
        in_specs=[smem, smem, smem, vmem, vmem, vmem, pl.BlockSpec(memory_space=pl.ANY)],
        out_specs=vmem,
        scratch_shapes=common + common_sems + recv + extra,
        compiler_params=pltpu.CompilerParams(
            collective_id=0, has_side_effects=True, vmem_limit_bytes=VMEM_BYTES
        ),
    )(
        pick, my_slot, counts, queries.reshape(tiles), keys.reshape(tiles), values.reshape(tiles),
        w_out,
    )


def solution(mesh):
    placed = (
        P("frames", "heads"),
        P("frames", "heads"),
        P("frames", "heads"),
        P(),
        P("frames"),
        P("heads", None),
    )
    return jax.shard_map(
        shards, mesh=mesh, in_specs=placed, out_specs=P("frames", "heads"), check_vma=False
    )
```

profile of v0, /device:TPU:0, one launch (start us, length us, event | category | flops | bytes accessed | tf_op | source)
XLA Modules:
  0.0 205.2 jit_solution(11120047719102744846)
XLA Ops:
  0.0 0.8 copy.8
  0.8 0.1 reshape.120
  0.9 0.1 convert_reduce_fusion
  1.0 0.2 select_reduce_fusion
  1.2 0.5 dynamic-slice_bitcast_fusion.slot_ref
  1.8 0.6 reshape.121.pick_ref
  2.4 199.4 %shard_map.64 = bf16[1024,1280]{1,0:T(8,128)(2,1)} custom-call(s32[256]{0:T(256)} %reshape.121.pick_ref, s32[32]{0:T(128)} %dynamic-slice_bitcast_fusion.slot_ref, s32[8]{0:T(128)} %count_ref.1, bf16[8,128,640]{2,1,0:T(8,128)(2,1)} %bitcast.5, bf16[8,128,640]{2,1,0:T(8,128)(2,1)} %bitcast.6, bf16[8,128,640]{2,1,0:T(8,128)(2,1)} %bitcast.7, ...), custom_call_target="tpu_custom_call" | custom-call | tf_op jit(solution)/shard_map/pallas_call | solution.py:435
  201.8 3.4 %copy.10 = bf16[1024,1280]{1,0:T(8,128)(2,1)} copy(bf16[1024,1280]{1,0:T(8,128)(2,1)} %shard_map.64) | data formatting | bytes 5242880
  (3 shorter events, 0.0 us)
where the time goes:
time: 205 us
  Pallas kernels  199 us (97%)
  local copies, waits for them, and re-layouts  5.42 us (3%)
    pallas_call x1, Pallas kernels, shards(): pl.pallas_call(functools.partial(layer_kernel, dims, relayed), out_shape=...  199 us
    unnamed x2, local copies, waits for them, and re-layouts  4.17 us

commit v1 on v0

--- a/solution.py
+++ b/solution.py
@@ -13,9 +13,14 @@
 MESH = pl.DeviceIdType.MESH
 F32 = jnp.float32
 PAIR = 2
+LINE = 4
 PARTS = 2
 UNROLL = 2
-AHEAD = 2
+EARLY = 3
+SUBLANES = 8
+LOG2E = math.log2(math.e)
+LOWEST = -1e38
+SMALLEST = 1e-37
 VMEM_BYTES = 67043328
 NT_DIMS = (((1,), (1,)), ((), ()))
 
@@ -92,137 +97,8 @@
             self.others(lambda target: self.copy(h, target, self.me_f).wait_send())
 
 
-class relay_exchange:
-    def __init__(
-        self, dims, pick_ref, k_ref, v_ref, recv,
-        picked, up_send, up_recv, down_send, down_recv, x_send, x_recv, *passing,
-    ):
-        self.frames, _, self.blocks, _, self.capacity, self.heads, _ = dims
-        self.line = self.frames // PAIR
-        self.pick_ref, self.k_ref, self.v_ref, self.recv = pick_ref, k_ref, v_ref, recv
-        self.picked, self.x_send, self.x_recv = picked, x_send, x_recv
-        self.sems = ((up_send, up_recv), (down_send, down_recv))
-        self.passing = passing
-        self.me_f, self.me_p = lax.axis_index("frames"), lax.axis_index("heads")
-        self.z, self.x = self.me_f // PAIR, self.me_f % PAIR
-        self.partner = self.z * PAIR + (PAIR - 1 - self.x)
-
-    def held(self, h, way, far):
-        return self.passing[(h * 2 + way) * (self.line - 1) + far - 1]
-
-    def at(self, way, steps):
-        return self.z + steps if way == 0 else self.z - steps
-
-    def inside(self, position):
-        return (position >= 0) & (position < self.line)
-
-    def onward(self, h, way, far, kv):
-        source = (self.k_ref, self.v_ref)[kv].at[:, :, head_columns(h)]
-        if far > 0:
-            source = self.held(h, way, far).at[kv]
-        send_sem, recv_sem = self.sems[way]
-        return pltpu.make_async_remote_copy(
-            src_ref=source,
-            dst_ref=self.held(h, way, far + 1).at[kv],
-            send_sem=send_sem.at[h, far, kv],
-            recv_sem=recv_sem.at[h, far, kv],
-            device_id=(self.at(way, 1) * PAIR + self.x, self.me_p),
-            device_id_type=MESH,
-        )
-
-    def beside(self, h, origin_z, column):
-        return pltpu.make_async_remote_copy(
-            src_ref=self.picked.at[h, origin_z],
-            dst_ref=self.recv[h].at[
-                pl.ds((origin_z * PAIR + column) * self.capacity, self.capacity)
-            ],
-            send_sem=self.x_send.at[h, origin_z],
-            recv_sem=self.x_recv.at[h, origin_z],
-            device_id=(self.partner, self.me_p),
-            device_id_type=MESH,
-        )
-
-    def send_on(self, h, way, far):
-        @pl.when(self.inside(self.at(way, 1)))
-        def _():
-            for kv in range(2):
-                self.onward(h, way, far, kv).start()
-
-    def hand_out(self, h, origin_z, load):
-        origin = origin_z * PAIR + self.x
-        for c in range(self.capacity):
-            theirs = self.pick_ref[(self.partner * self.frames + origin) * self.capacity + c]
-            for kv in range(2):
-                self.picked[h, origin_z, c, kv] = load(kv, theirs)
-        for c in range(self.capacity):
-            ours = self.pick_ref[(self.me_f * self.frames + origin) * self.capacity + c]
-            for kv in range(2):
-                self.recv[h][origin * self.capacity + c, kv] = load(kv, ours)
-        self.beside(h, origin_z, self.x).start()
-
-    def own(self, h):
-        def load(kv, index):
-            return (self.k_ref, self.v_ref)[kv][index, :, head_columns(h)]
-
-        self.hand_out(h, self.z, load)
-
-    def arrive(self, h, far):
-        for way in range(2):
-            @pl.when(self.inside(self.at(way, -far)))
-            def _():
-                for kv in range(2):
-                    self.onward(h, way, far - 1, kv).wait_recv()
-                if far + 1 < self.line:
-                    self.send_on(h, way, far)
-
-        for way in range(2):
-            @pl.when(self.inside(self.at(way, -far)))
-            def _():
-                held = self.held(h, way, far)
-                self.hand_out(h, self.at(way, -far), lambda kv, index: held[kv, index])
-
-    def prepare(self):
-        pass
-
-    def begin(self):
-        for h in range(min(AHEAD, self.heads)):
-            for way in range(2):
-                self.send_on(h, way, 0)
-
-    def follow(self):
-        self.own(0)
-
-    def receive(self, h, midway):
-        for far in range(1, self.line):
-            if far == self.line - 1:
-                midway()
-            self.arrive(h, far)
-            if far == 1 and h + AHEAD < self.heads:
-                for way in range(2):
-                    self.send_on(h + AHEAD, way, 0)
-        if h + 1 < self.heads:
-            self.own(h + 1)
-
-        @pl.loop(0, self.line)
-        def _(origin_z):
-            self.beside(h, origin_z, PAIR - 1 - self.x).wait_recv()
-
-    def drain(self):
-        for h in range(self.heads):
-            for way in range(2):
-                for far in range(self.line - 1):
-                    @pl.when(self.inside(self.at(way, -far)) & self.inside(self.at(way, 1)))
-                    def _():
-                        for kv in range(2):
-                            self.onward(h, way, far, kv).wait_send()
-
-            @pl.loop(0, self.line)
-            def _(origin_z):
-                self.beside(h, origin_z, self.x).wait_send()
-
-
 def layer_kernel(
-    dims, relayed, pick_ref, slot_ref, count_ref, q_ref, k_ref, v_ref, w_ref, out_ref,
+    dims, pick_ref, slot_ref, count_ref, q_ref, k_ref, v_ref, w_ref, out_ref,
     rows, attn, acc, w_send, w_recv, a_send, a_recv, own_sem, *kv_refs,
 ):
     frames, peers, blocks, select, capacity, heads, slots = dims
@@ -251,9 +127,7 @@
     own_rows = pltpu.make_async_copy(w_ref.at[:, columns_of(me_p)], rows.at[me_p], own_sem)
     own_rows.start()
 
-    exchange = (relay_exchange if relayed else direct_exchange)(
-        dims, pick_ref, k_ref, v_ref, recv, *kv_refs
-    )
+    exchange = direct_exchange(dims, pick_ref, k_ref, v_ref, recv, *kv_refs)
 
     def w_copy(target, origin):
         return pltpu.make_async_remote_copy(
@@ -404,7 +278,6 @@
     tiles = (blocks, TILE, width)
     dma = pltpu.SemaphoreType.DMA
     bf16 = jnp.bfloat16
-    line = frames // PAIR
     common = [
         pltpu.VMEM((peers, width, features), bf16),
         pltpu.VMEM((heads, peers, tokens, DH), bf16),
@@ -415,25 +288,14 @@
         dma((heads, PARTS, peers)), dma,
     ]
     recv = [pltpu.VMEM((frames * capacity, 2, TILE, DH), bf16)] * heads
-    picked = pltpu.VMEM((heads, line, capacity, 2, TILE, DH), bf16)
-    passing = [pltpu.VMEM((2, blocks, TILE, DH), bf16)] * (heads * 2 * (line - 1))
-    operands = tokens * (3 * width + features) * 2
-    needed = operands + sum(
-        math.prod(m.shape) * jnp.dtype(m.dtype).itemsize
-        for m in common + recv + [picked] + passing
-    )
-    relayed = frames % PAIR == 0 and needed < VMEM_BYTES * 15 // 16
-    if relayed:
-        extra = [picked] + [dma((heads, line, 2))] * 4 + [dma((heads, line))] * 2 + passing
-    else:
-        extra = [
-            pltpu.VMEM((slots, frames, capacity, 2, TILE, DH), bf16),
-            dma((heads, frames)),
-            dma((heads, frames)),
-        ]
+    extra = [
+        pltpu.VMEM((slots, frames, capacity, 2, TILE, DH), bf16),
+        dma((heads, frames)),
+        dma((heads, frames)),
+    ]
     dims = (frames, peers, blocks, select, capacity, heads, slots)
     return pl.pallas_call(
-        functools.partial(layer_kernel, dims, relayed),
+        functools.partial(layer_kernel, dims),
         out_shape=jax.ShapeDtypeStruct((tokens, features), bf16),
         in_specs=[smem, smem, smem, vmem, vmem, vmem, pl.BlockSpec(memory_space=pl.ANY)],
         out_specs=vmem,
@@ -447,6 +309,454 @@
     )
 
 
+def column_kernel(
+    dims, ids_ref, own_count_ref, q_ref, k_ref, v_ref, w_ref, out_ref,
+    rows, attn, acc, qall, count, osend, orecv, ssend, srecv, oself, sself, place, usable,
+    w_send, w_recv, a_send, a_recv, own_sem, kv_send, kv_recv, q_send, q_recv,
+    c_send, c_recv, o_send, o_recv, s_send, s_recv, *kv,
+):
+    frames, peers, blocks, select, heads = dims
+    me_f, me_p = lax.axis_index("frames"), lax.axis_index("heads")
+    line = frames // PAIR
+    z, x = me_f // PAIR, me_f % PAIR
+    half = z // (line // 2)
+    mid, end = half + 1, (line - 1) * half
+    across = line - 1 - mid
+    is_mid = z == mid
+    is_end = z == end
+    other = 1 - x
+    depth = heads * DH
+    features = rows.shape[2]
+    part_blocks = blocks // PARTS
+    part_rows = part_blocks * TILE
+    exponent = LOG2E / DH**0.5
+
+    def at(zz, xx):
+        return (zz * PAIR + xx, me_p)
+
+    barrier = pltpu.get_barrier_semaphore()
+
+    @pl.loop(1, frames)
+    def _(step):
+        pl.semaphore_signal(
+            barrier, inc=1, device_id=(lax.rem(me_f + step, frames), me_p), device_id_type=MESH
+        )
+
+    @pl.loop(1, peers)
+    def _(step):
+        pl.semaphore_signal(
+            barrier, inc=1, device_id=(me_f, lax.rem(me_p + step, peers)), device_id_type=MESH
+        )
+
+    def columns_of(peer):
+        return pl.ds(pl.multiple_of(peer * features, features), features)
+
+    own_rows = pltpu.make_async_copy(w_ref.at[:, columns_of(me_p)], rows.at[me_p], own_sem)
+    own_rows.start()
+
+    def send(source, target, send_sem, recv_sem, device):
+        return pltpu.make_async_remote_copy(
+            src_ref=source, dst_ref=target, send_sem=send_sem, recv_sem=recv_sem,
+            device_id=device, device_id_type=MESH,
+        )
+
+    def kv_copy(h, flow, which):
+        source = (k_ref, v_ref)[which].at[:, :, head_columns(h)]
+        if flow == 2:
+            source = kv[h].at[which, pl.ds(blocks, blocks)]
+        return send(
+            source, kv[h].at[which, pl.ds((flow + 1) * blocks, blocks)],
+            kv_send.at[flow, h, which], kv_recv.at[flow, h, which],
+            at(mid, x) if flow == 0 else at(across, x),
+        )
+
+    def q_copy(h, flow):
+        source = q_ref.at[:, :, head_columns(h)] if flow < 2 else qall.at[h, 1]
+        return send(
+            source, qall.at[h, flow], q_send.at[flow, h], q_recv.at[flow, h],
+            at(mid, x) if flow == 1 else at(z, other),
+        )
+
+    def c_copy(flow):
+        device = (at(z, other), at(mid, x), at(mid, other))[flow]
+        return send(
+            own_count_ref, count.at[flow + 1], c_send.at[flow], c_recv.at[flow], device
+        )
+
+    def o_copies(h, part, slot):
+        span = pl.ds(part * part_rows, part_rows)
+        to_z = z + (end - z) * ((slot + 1) // 2)
+        to_x = x + (other - x) * ((slot + 1) % 2)
+        device = at(to_z, to_x)
+        return (
+            send(
+                osend.at[h, slot, span], orecv.at[h, slot, span],
+                o_send.at[h, part, slot], o_recv.at[h, part, slot], device,
+            ),
+            send(
+                ssend.at[h, slot, part], srecv.at[h, slot, part],
+                s_send.at[h, part, slot], s_recv.at[h, part, slot], device,
+            ),
+        )
+
+    def w_copy(h, target, origin):
+        span = pl.ds(h * DH, DH)
+        return send(
+            w_ref.at[span, columns_of(target)], rows.at[origin, span],
+            w_send.at[h, target], w_recv.at[h, origin], (me_f, target),
+        )
+
+    def a_copy(h, part, target, origin):
+        held = attn.at[h, origin, pl.ds(part * part_rows, part_rows)]
+        return send(
+            held, held, a_send.at[h, part, target, origin], a_recv.at[h, part, origin],
+            (me_f, target),
+        )
+
+    twin = me_p + 1 - 2 * lax.rem(me_p, 2)
+
+    def over_peers(action):
+        @pl.loop(1, peers)
+        def _(step):
+            action(lax.rem(me_p + step, peers))
+
+    def over_alike(action):
+        @pl.loop(1, peers // 2)
+        def _(step):
+            action(lax.rem(me_p + 2 * step, peers))
+
+    def over_twins(action):
+        @pl.loop(0, peers // 2)
+        def _(step):
+            action(lax.rem(twin + 2 * step, peers))
+
+    def share(h, part):
+        over_alike(lambda target: a_copy(h, part, target, me_p).start())
+        a_copy(h, part, twin, me_p).start()
+
+    def finish(h):
+        if h == 0:
+            own_rows.wait()
+        over_peers(lambda origin: w_copy(h, origin, origin).wait_recv())
+        for part in range(PARTS):
+
+            def relay(origin):
+                a_copy(h, part, origin, origin).wait_recv()
+                a_copy(h, part, twin, origin).start()
+
+            over_alike(relay)
+        for part in range(PARTS):
+            over_twins(lambda origin: a_copy(h, part, origin, origin).wait_recv())
+            project(h, part)
+
+    def drain_attn(h, part):
+        over_alike(lambda target: a_copy(h, part, target, me_p).wait_send())
+        a_copy(h, part, twin, me_p).wait_send()
+        over_alike(lambda origin: a_copy(h, part, twin, origin).wait_send())
+
+    row_tile = 2 * TILE
+
+    def project(h, part):
+        @pl.loop(part * part_rows // row_tile, (part + 1) * part_rows // row_tile)
+        def _(r):
+            span = pl.ds(pl.multiple_of(r * row_tile, row_tile), row_tile)
+            left = jnp.concatenate([attn[h, p, span, :] for p in range(peers)], axis=1)
+            right = jnp.concatenate([rows[p, head_columns(h), :] for p in range(peers)], axis=0)
+            term = jnp.dot(left, right, preferred_element_type=F32)
+            if h > 0:
+                term = term + acc[span, :]
+            if h == heads - 1:
+                out_ref[span, :] = term.astype(out_ref.dtype)
+            else:
+                acc[span, :] = term
+
+    def fill_tables():
+        for role in range(4):
+            role_z = z if role < 2 else end
+            role_x = x if role % 2 == 0 else other
+
+            @pl.loop(0, blocks)
+            def _(b):
+                for s in range(select):
+                    chosen = ids_ref[s, (role_z * PAIR + role_x) * blocks + b]
+                    owner = lax.div(chosen, blocks)
+                    owner_z, owner_x = lax.div(owner, PAIR), lax.rem(owner, PAIR)
+                    here = owner_z == z
+                    near = owner_z == end
+                    source = jnp.where(
+                        here, 0, jnp.where(near, 1, jnp.where(owner_z == across, 2, 3))
+                    )
+                    ours = here | is_mid
+                    if role > 1:
+                        ours = ours & jnp.logical_not(near)
+                    ours = ours & (owner_x == x)
+                    entry = (role * blocks + b) * select + s
+                    index = source * blocks + lax.rem(chosen, blocks)
+                    place[entry] = jnp.where(ours, index, 0)
+                    usable[entry] = jnp.where(ours, 1, 0)
+
+    def own_block(h):
+        @pl.loop(0, blocks)
+        def _(b):
+            kv[h][0, b] = k_ref[b, :, head_columns(h)]
+            kv[h][1, b] = v_ref[b, :, head_columns(h)]
+
+    lane = lax.broadcasted_iota(jnp.int32, (TILE, TILE), 1)
+
+    def partial(h, role, b, query, first_keys, first_values):
+        entries = [(role * blocks + b) * select + s for s in range(select)]
+        picks = [place[e] for e in entries]
+        keyset = jnp.concatenate(first_keys + [kv[h][0, i] for i in picks], axis=0)
+        valueset = jnp.concatenate(first_values + [kv[h][1, i] for i in picks], axis=0)
+        scores = lax.dot_general(query, keyset, NT_DIMS, preferred_element_type=F32)
+        used = count[role, pl.ds(b, 1), :]
+        pieces = [scores[:, i * TILE : (i + 1) * TILE] for i in range(len(first_keys) + select)]
+        for s in range(select):
+            keep = jnp.broadcast_to(used * usable[entries[s]], (TILE, TILE)) > s
+            at_piece = len(first_keys) + s
+            pieces[at_piece] = jnp.where(keep, pieces[at_piece], -jnp.inf)
+        top = jnp.max(functools.reduce(jnp.maximum, pieces), axis=1, keepdims=True)
+        top = jnp.maximum(top, LOWEST)
+        probs = [jnp.exp2((piece - top) * exponent) for piece in pieces]
+        denom = jnp.sum(functools.reduce(jnp.add, probs), axis=1, keepdims=True)
+        weights = jnp.concatenate([p.astype(jnp.bfloat16) for p in probs], axis=1)
+        mixed = jnp.dot(weights, valueset, preferred_element_type=F32)
+        level = top * exponent + jnp.log(denom) * LOG2E
+        return mixed / jnp.maximum(denom, SMALLEST), level
+
+    def rows_of(levels):
+        tile = jnp.zeros((TILE, TILE), F32)
+        for j, level in enumerate(levels):
+            tile = jnp.where(lane == j, level, tile)
+        return tile.T[:SUBLANES]
+
+    others = 1 + 2 * is_mid.astype(jnp.int32)
+
+    def attend_others(h):
+        @pl.loop(0, PARTS * others)
+        def _(step):
+            part, turn = step // others, step % others
+            role = others - turn
+            levels = []
+            for j in range(part_blocks):
+                b = part * part_blocks + j
+                mixed, level = partial(h, role, b, qall[h, role - 1, b], [], [])
+                span = pl.ds(pl.multiple_of(b * TILE, TILE), TILE)
+                osend[h, role - 1, span, :] = mixed.astype(jnp.bfloat16)
+                levels.append(level)
+            ssend[h, role - 1, part] = rows_of(levels)
+            for copy in o_copies(h, part, role - 1):
+                copy.start()
+            if h + 1 < heads:
+
+                @pl.when(is_mid & (step == others - 1))
+                def _():
+                    relay_on(h + 1)
+
+    def attend_own(h):
+        @pl.loop(0, PARTS)
+        def _(part):
+            levels = []
+            for j in range(part_blocks):
+                b = part * part_blocks + j
+                mixed, level = partial(
+                    h, 0, b, q_ref[b, :, head_columns(h)],
+                    [k_ref[b, :, head_columns(h)]], [v_ref[b, :, head_columns(h)]],
+                )
+                oself[pl.ds(pl.multiple_of(b * TILE, TILE), TILE), :] = mixed
+                levels.append(level)
+            sself[part] = rows_of(levels)
+
+    def merge(h, part, slots):
+        levels = [sself[part]] + [srecv[h, slot, part] for slot in range(slots)]
+        top = functools.reduce(jnp.maximum, levels)
+        shares = [jnp.exp2(level - top) for level in levels]
+        total = functools.reduce(jnp.add, shares)
+        spare = TILE - SUBLANES * len(shares)
+        tall = jnp.concatenate(
+            [share / total for share in shares] + [jnp.zeros((spare, TILE), F32)], axis=0
+        ).T
+        for j in range(part_blocks):
+            span = pl.ds((part * part_blocks + j) * TILE, TILE)
+            value = oself[span, :] * tall[:, j : j + 1]
+            for slot in range(slots):
+                column = SUBLANES * (slot + 1) + j
+                value = value + orecv[h, slot, span, :].astype(F32) * tall[:, column : column + 1]
+            attn[h, me_p, span, :] = value.astype(jnp.bfloat16)
+
+    def combine(h, part):
+        for copy in o_copies(h, part, 0):
+            copy.wait_recv()
+
+        @pl.when(is_mid)
+        def _():
+            merge(h, part, 1)
+
+        @pl.when(is_end)
+        def _():
+            for slot in (1, 2):
+                for copy in o_copies(h, part, slot):
+                    copy.wait_recv()
+            merge(h, part, 3)
+
+    def relay_on(h):
+        for which in range(2):
+            kv_copy(h, 0, which).wait_recv()
+            kv_copy(h, 2, which).start()
+        if h + 1 < heads:
+            for which in range(2):
+                kv_copy(h + 1, 1, which).start()
+        q_copy(h, 1).wait_recv()
+        q_copy(h, 2).start()
+
+    def send_early(h):
+        q_copy(h, 0).start()
+
+        @pl.when(is_end)
+        def _():
+            for which in range(2):
+                kv_copy(h, 0, which).start()
+            q_copy(h, 1).start()
+
+    def send_rows(h):
+        over_peers(lambda target: w_copy(h, target, me_p).start())
+
+    pl.semaphore_wait(barrier, frames + peers - 2)
+    c_copy(0).start()
+
+    @pl.when(is_end)
+    def _():
+        c_copy(1).start()
+        c_copy(2).start()
+
+    @pl.when(is_mid)
+    def _():
+        for which in range(2):
+            kv_copy(0, 1, which).start()
+
+    for h in range(min(EARLY, heads)):
+        send_early(h)
+        send_rows(h)
+    count[0] = own_count_ref[...]
+    fill_tables()
+    own_block(0)
+    c_copy(0).wait_recv()
+
+    @pl.when(is_mid)
+    def _():
+        relay_on(0)
+        c_copy(1).wait_recv()
+        c_copy(2).wait_recv()
+
+    for h in range(heads):
+        if h + EARLY < heads:
+            send_early(h + EARLY)
+        if h > 0:
+            own_block(h)
+        q_copy(h, 0).wait_recv()
+
+        @pl.when(is_mid)
+        def _():
+            for which in range(2):
+                kv_copy(h, 1, which).wait_recv()
+                kv_copy(h, 2, which).wait_recv()
+            q_copy(h, 2).wait_recv()
+
+        attend_others(h)
+        attend_own(h)
+        if h > 0:
+            finish(h - 1)
+        for part in range(PARTS):
+            combine(h, part)
+            share(h, part)
+        if h + EARLY < heads:
+            send_rows(h + EARLY)
+    finish(heads - 1)
+
+    c_copy(0).wait_send()
+
+    @pl.when(is_end)
+    def _():
+        c_copy(1).wait_send()
+        c_copy(2).wait_send()
+
+    for h in range(heads):
+        over_peers(lambda target: w_copy(h, target, me_p).wait_send())
+        q_copy(h, 0).wait_send()
+
+        @pl.when(is_end)
+        def _():
+            for which in range(2):
+                kv_copy(h, 0, which).wait_send()
+            q_copy(h, 1).wait_send()
+
+        @pl.when(is_mid)
+        def _():
+            for which in range(2):
+                kv_copy(h, 1, which).wait_send()
+                kv_copy(h, 2, which).wait_send()
+            q_copy(h, 2).wait_send()
+
+        for part in range(PARTS):
+            drain_attn(h, part)
+
+            @pl.loop(0, others)
+            def _(slot):
+                for copy in o_copies(h, part, slot):
+                    copy.wait_send()
+
+
+def column_shards(queries, keys, values, block_ids, counts, w_out):
+    frames = lax.axis_size("frames")
+    peers = lax.axis_size("heads")
+    tokens, width = queries.shape
+    blocks = tokens // TILE
+    select = block_ids.shape[1]
+    heads = width // DH
+    features = w_out.shape[1] // peers
+    smem = pl.BlockSpec(memory_space=pltpu.SMEM)
+    vmem = pl.BlockSpec(memory_space=pltpu.VMEM)
+    tiles = (blocks, TILE, width)
+    dma = pltpu.SemaphoreType.DMA
+    bf16 = jnp.bfloat16
+    level_rows = (PARTS, SUBLANES, TILE)
+    scratch = [
+        pltpu.VMEM((peers, width, features), bf16),
+        pltpu.VMEM((heads, peers, tokens, DH), bf16),
+        pltpu.VMEM((tokens, features), F32),
+        pltpu.VMEM((heads, 3, blocks, TILE, DH), bf16),
+        pltpu.VMEM((4, blocks, TILE), jnp.int32),
+        pltpu.VMEM((heads, 3, tokens, DH), bf16),
+        pltpu.VMEM((heads, 3, tokens, DH), bf16),
+        pltpu.VMEM((heads, 3) + level_rows, F32),
+        pltpu.VMEM((heads, 3) + level_rows, F32),
+        pltpu.VMEM((tokens, DH), F32),
+        pltpu.VMEM(level_rows, F32),
+        pltpu.SMEM((4 * blocks * select,), jnp.int32),
+        pltpu.SMEM((4 * blocks * select,), jnp.int32),
+        dma((heads, peers)), dma((heads, peers)), dma((heads, PARTS, peers, peers)),
+        dma((heads, PARTS, peers)), dma,
+        dma((3, heads, 2)), dma((3, heads, 2)), dma((3, heads)), dma((3, heads)),
+        dma((3,)), dma((3,)),
+        dma((heads, PARTS, 3)), dma((heads, PARTS, 3)),
+        dma((heads, PARTS, 3)), dma((heads, PARTS, 3)),
+    ] + [pltpu.VMEM((2, 4 * blocks, TILE, DH), bf16)] * heads
+    dims = (frames, peers, blocks, select, heads)
+    return pl.pallas_call(
+        functools.partial(column_kernel, dims),
+        out_shape=jax.ShapeDtypeStruct((tokens, features), bf16),
+        in_specs=[smem, vmem, vmem, vmem, vmem, pl.BlockSpec(memory_space=pl.ANY)],
+        out_specs=vmem,
+        scratch_shapes=scratch,
+        compiler_params=pltpu.CompilerParams(
+            collective_id=0, has_side_effects=True, vmem_limit_bytes=VMEM_BYTES
+        ),
+    )(
+        block_ids.T, jnp.broadcast_to(counts[:, None], (blocks, TILE)),
+        queries.reshape(tiles), keys.reshape(tiles), values.reshape(tiles), w_out,
+    )
+
+
 def solution(mesh):
     placed = (
         P("frames", "heads"),
@@ -456,6 +766,7 @@
         P("frames"),
         P("heads", None),
     )
+    columns = mesh.shape["frames"] == PAIR * LINE and mesh.shape["heads"] % 2 == 0
     return jax.shard_map(
-        shards, mesh=mesh, in_specs=placed, out_specs=P("frames", "heads"), check_vma=False
+        column_shards if columns else shards, mesh=mesh, in_specs=placed, out_specs=P("frames", "heads"), check_vma=False
     )

time: 205 us -> 154 us (0.75)
  Pallas kernels: 199 us -> 148 us
    pallas_call x1, Pallas kernels: 199 us -> 148 us  [column_shards(): pl.pallas_call(functools.partial(column_kernel, dims), out_shape=jax.Shap...]
    unnamed x2 -> x1, local copies, waits for them, and re-layouts: 4.17 us -> 3.4 us
where the time goes in v1:
time: 154 us; the launch traced here: 152 us
  Pallas kernels  148 us (96%)
  local copies, waits for them, and re-layouts  4.72 us (3%)
    pallas_call x1, Pallas kernels, column_shards(): pl.pallas_call(functools.partial(column_kernel, dims), out_shape=jax.Shap...  148 us
    unnamed x1, local copies, waits for them, and re-layouts  3.4 us

profile of v1, /device:TPU:0, one launch (start us, length us, event | category | flops | bytes accessed | tf_op | source)
XLA Modules:
  0.0 152.4 jit_solution(11936237760450983203)
XLA Ops:
  0.0 1.3 broadcast_in_dim.2.own_count_ref
  1.3 147.7 %shard_map.64 = bf16[1024,1280]{1,0:T(8,128)(2,1)} custom-call(s32[4,64]{1,0:T(4,128)} %bitcast.7, s32[8,128]{1,0:T(8,128)} %broadcast_in_dim.2.own_count_ref, bf16[8,128,640]{2,1,0:T(8,128)(2,1)} %bitcast.4, bf16[8,128,640]{2,1,0:T(8,128)(2,1)} %bitcast.5, bf16[8,128,640]{2,1,0:T(8,128)(2,1)} %bitcast.6, bf16[640,5120]{1,0:T(8,128)(2,1)} %w_ref.1), custom_call_target="tpu_custom_call" | custom-call | tf_op jit(solution)/shard_map/pallas_call | solution.py:745
  149.0 3.4 %copy.8 = bf16[1024,1280]{1,0:T(8,128)(2,1)} copy(bf16[1024,1280]{1,0:T(8,128)(2,1)} %shard_map.64) | data formatting | bytes 5242880

commit v2 on v1

--- a/solution.py
+++ b/solution.py
@@ -17,10 +17,8 @@
 PARTS = 2
 UNROLL = 2
 EARLY = 3
-SUBLANES = 8
 LOG2E = math.log2(math.e)
 LOWEST = -1e38
-SMALLEST = 1e-37
 VMEM_BYTES = 67043328
 NT_DIMS = (((1,), (1,)), ((), ()))
 
@@ -310,12 +308,13 @@
 
 
 def column_kernel(
-    dims, ids_ref, own_count_ref, q_ref, k_ref, v_ref, w_ref, out_ref,
-    rows, attn, acc, qall, count, osend, orecv, ssend, srecv, oself, sself, place, usable,
-    w_send, w_recv, a_send, a_recv, own_sem, kv_send, kv_recv, q_send, q_recv,
-    c_send, c_recv, o_send, o_recv, s_send, s_recv, *kv,
+    dims, ids_ref, own_count_ref, q_hbm, k_hbm, v_hbm, w_ref, out_ref,
+    q_ref, k_ref, v_ref, rows, attn, acc, qall, count, osend, orecv, ssend, srecv, oself, sself, weights, finished, place, usable,
+    w_send, w_recv, a_send, a_recv, own_sem, load_sem, turn_sem, out_sem,
+    kv_send, kv_recv, q_send, q_recv, c_send, c_recv, o_send, o_recv, s_send, s_recv, *kv,
 ):
     frames, peers, blocks, select, heads = dims
+    keys, values = kv[:heads], kv[heads:]
     me_f, me_p = lax.axis_index("frames"), lax.axis_index("heads")
     line = frames // PAIR
     z, x = me_f // PAIR, me_f % PAIR
@@ -334,25 +333,38 @@
     def at(zz, xx):
         return (zz * PAIR + xx, me_p)
 
+    loads = [
+        pltpu.make_async_copy(source, held, load_sem.at[i])
+        for i, (source, held) in enumerate(((k_hbm, k_ref), (v_hbm, v_ref), (q_hbm, q_ref)))
+    ]
+    for load in loads:
+        load.start()
     barrier = pltpu.get_barrier_semaphore()
 
-    @pl.loop(1, frames)
-    def _(step):
-        pl.semaphore_signal(
-            barrier, inc=1, device_id=(lax.rem(me_f + step, frames), me_p), device_id_type=MESH
-        )
+    def greet(device):
+        pl.semaphore_signal(barrier, inc=1, device_id=device, device_id_type=MESH)
 
     @pl.loop(1, peers)
     def _(step):
-        pl.semaphore_signal(
-            barrier, inc=1, device_id=(me_f, lax.rem(me_p + step, peers)), device_id_type=MESH
-        )
+        greet((me_f, lax.rem(me_p + step, peers)))
+
+    greet(at(z, other))
+    greet(at(mid + end - z, x))
+    greet(at(mid + end - z, other))
+
+    @pl.when(is_mid)
+    def _():
+        greet(at(across, x))
 
     def columns_of(peer):
         return pl.ds(pl.multiple_of(peer * features, features), features)
 
     own_rows = pltpu.make_async_copy(w_ref.at[:, columns_of(me_p)], rows.at[me_p], own_sem)
     own_rows.start()
+
+    @pl.loop(0, blocks)
+    def _(b):
+        count[0, pl.ds(b, 1), :] = jnp.full((1, TILE), own_count_ref[b], jnp.int32)
 
     def send(source, target, send_sem, recv_sem, device):
         return pltpu.make_async_remote_copy(
@@ -361,11 +373,12 @@
         )
 
     def kv_copy(h, flow, which):
+        held = (keys, values)[which][h]
         source = (k_ref, v_ref)[which].at[:, :, head_columns(h)]
         if flow == 2:
-            source = kv[h].at[which, pl.ds(blocks, blocks)]
+            source = held.at[pl.ds(blocks, blocks)]
         return send(
-            source, kv[h].at[which, pl.ds((flow + 1) * blocks, blocks)],
+            source, held.at[pl.ds((flow + 1) * blocks, blocks)],
             kv_send.at[flow, h, which], kv_recv.at[flow, h, which],
             at(mid, x) if flow == 0 else at(across, x),
         )
@@ -380,23 +393,25 @@
     def c_copy(flow):
         device = (at(z, other), at(mid, x), at(mid, other))[flow]
         return send(
-            own_count_ref, count.at[flow + 1], c_send.at[flow], c_recv.at[flow], device
-        )
-
-    def o_copies(h, part, slot):
-        span = pl.ds(part * part_rows, part_rows)
+            count.at[0], count.at[flow + 1], c_send.at[flow], c_recv.at[flow], device
+        )
+
+    def partial_device(slot):
         to_z = z + (end - z) * ((slot + 1) // 2)
         to_x = x + (other - x) * ((slot + 1) % 2)
-        device = at(to_z, to_x)
-        return (
-            send(
-                osend.at[h, slot, span], orecv.at[h, slot, span],
-                o_send.at[h, part, slot], o_recv.at[h, part, slot], device,
-            ),
-            send(
-                ssend.at[h, slot, part], srecv.at[h, slot, part],
-                s_send.at[h, part, slot], s_recv.at[h, part, slot], device,
-            ),
+        return at(to_z, to_x)
+
+    def o_copy(h, part, slot):
+        span = pl.ds(part * part_rows, part_rows)
+        return send(
+            osend.at[h, slot, span], orecv.at[h, slot, span],
+            o_send.at[h, part, slot], o_recv.at[h, part, slot], partial_device(slot),
+        )
+
+    def s_copy(h, slot):
+        return send(
+            ssend.at[h, slot], srecv.at[h, slot], s_send.at[h, slot], s_recv.at[h, slot],
+            partial_device(slot),
         )
 
     def w_copy(h, target, origin):
@@ -408,8 +423,10 @@
 
     def a_copy(h, part, target, origin):
         held = attn.at[h, origin, pl.ds(part * part_rows, part_rows)]
+        to_twin = lax.rem(target + me_p, 2)
+        lane_of = target + to_twin * (origin - me_p)
         return send(
-            held, held, a_send.at[h, part, target, origin], a_recv.at[h, part, origin],
+            held, held, a_send.at[h, part, lane_of], a_recv.at[h, part, origin],
             (me_f, target),
         )
 
@@ -433,19 +450,21 @@
     def share(h, part):
         over_alike(lambda target: a_copy(h, part, target, me_p).start())
         a_copy(h, part, twin, me_p).start()
+
+    def pass_on(h):
+        for part in range(PARTS):
+
+            def relay(origin):
+                a_copy(h, part, origin, origin).wait_recv()
+                a_copy(h, part, twin, origin).start()
+
+            over_alike(relay)
 
     def finish(h):
         if h == 0:
             own_rows.wait()
         over_peers(lambda origin: w_copy(h, origin, origin).wait_recv())
         for part in range(PARTS):
-
-            def relay(origin):
-                a_copy(h, part, origin, origin).wait_recv()
-                a_copy(h, part, twin, origin).start()
-
-            over_alike(relay)
-        for part in range(PARTS):
             over_twins(lambda origin: a_copy(h, part, origin, origin).wait_recv())
             project(h, part)
 
@@ -455,6 +474,10 @@
         over_alike(lambda origin: a_copy(h, part, twin, origin).wait_send())
 
     row_tile = 2 * TILE
+
+    def out_copy(r):
+        span = pl.ds(pl.multiple_of(r * row_tile, row_tile), row_tile)
+        return pltpu.make_async_copy(finished.at[span], out_ref.at[span], out_sem.at[r])
 
     def project(h, part):
         @pl.loop(part * part_rows // row_tile, (part + 1) * part_rows // row_tile)
@@ -466,7 +489,8 @@
             if h > 0:
                 term = term + acc[span, :]
             if h == heads - 1:
-                out_ref[span, :] = term.astype(out_ref.dtype)
+                finished[span, :] = term.astype(out_ref.dtype)
+                out_copy(r).start()
             else:
                 acc[span, :] = term
 
@@ -498,81 +522,104 @@
     def own_block(h):
         @pl.loop(0, blocks)
         def _(b):
-            kv[h][0, b] = k_ref[b, :, head_columns(h)]
-            kv[h][1, b] = v_ref[b, :, head_columns(h)]
+            keys[h][b] = k_ref[b, :, head_columns(h)]
+            values[h][b] = v_ref[b, :, head_columns(h)]
 
     lane = lax.broadcasted_iota(jnp.int32, (TILE, TILE), 1)
 
-    def partial(h, role, b, query, first_keys, first_values):
+    def weigh(h, role, b, query, first_keys):
         entries = [(role * blocks + b) * select + s for s in range(select)]
-        picks = [place[e] for e in entries]
-        keyset = jnp.concatenate(first_keys + [kv[h][0, i] for i in picks], axis=0)
-        valueset = jnp.concatenate(first_values + [kv[h][1, i] for i in picks], axis=0)
+        keyset = jnp.concatenate(first_keys + [keys[h][place[e]] for e in entries], axis=0)
         scores = lax.dot_general(query, keyset, NT_DIMS, preferred_element_type=F32)
         used = count[role, pl.ds(b, 1), :]
-        pieces = [scores[:, i * TILE : (i + 1) * TILE] for i in range(len(first_keys) + select)]
+        lead = len(first_keys)
+        pieces = [scores[:, i * TILE : (i + 1) * TILE] for i in range(lead + select)]
         for s in range(select):
             keep = jnp.broadcast_to(used * usable[entries[s]], (TILE, TILE)) > s
-            at_piece = len(first_keys) + s
-            pieces[at_piece] = jnp.where(keep, pieces[at_piece], -jnp.inf)
+            pieces[lead + s] = jnp.where(keep, pieces[lead + s], -jnp.inf)
         top = jnp.max(functools.reduce(jnp.maximum, pieces), axis=1, keepdims=True)
         top = jnp.maximum(top, LOWEST)
         probs = [jnp.exp2((piece - top) * exponent) for piece in pieces]
         denom = jnp.sum(functools.reduce(jnp.add, probs), axis=1, keepdims=True)
-        weights = jnp.concatenate([p.astype(jnp.bfloat16) for p in probs], axis=1)
-        mixed = jnp.dot(weights, valueset, preferred_element_type=F32)
-        level = top * exponent + jnp.log(denom) * LOG2E
-        return mixed / jnp.maximum(denom, SMALLEST), level
+        for i, piece in enumerate(probs):
+            weights[role, b, :, i * TILE : (i + 1) * TILE] = piece.astype(jnp.bfloat16)
+        return top * exponent, denom
+
+    def mix(h, role, b, first_values):
+        entries = [(role * blocks + b) * select + s for s in range(select)]
+        valueset = jnp.concatenate(first_values + [values[h][place[e]] for e in entries], axis=0)
+        held = weights[role, b, :, : (len(first_values) + select) * TILE]
+        return jnp.dot(held, valueset, preferred_element_type=F32)
 
     def rows_of(levels):
         tile = jnp.zeros((TILE, TILE), F32)
-        for j, level in enumerate(levels):
-            tile = jnp.where(lane == j, level, tile)
-        return tile.T[:SUBLANES]
-
-    others = 1 + 2 * is_mid.astype(jnp.int32)
-
-    def attend_others(h):
-        @pl.loop(0, PARTS * others)
+        for j, (top, denom) in enumerate(levels):
+            tile = jnp.where(lane == j, top, tile)
+            tile = jnp.where(lane == part_blocks + j, denom, tile)
+        return tile.T[: 2 * part_blocks]
+
+    away = is_mid.astype(jnp.int32)
+
+    def over_others(action):
+        first = 2 * PARTS
+
+        @pl.loop(first * (1 - away), first + PARTS)
         def _(step):
-            part, turn = step // others, step % others
-            role = others - turn
+            late = step // first
+            role = late + (1 - late) * (3 - step % 2)
+            part = late * (step - first) + (1 - late) * (step // 2)
+            action(step, role, part)
+
+    def weigh_others(h):
+        def action(step, role, part):
             levels = []
             for j in range(part_blocks):
                 b = part * part_blocks + j
-                mixed, level = partial(h, role, b, qall[h, role - 1, b], [], [])
+                levels.append(weigh(h, role, b, qall[h, role - 1, b], []))
+            ssend[h, role - 1, part] = rows_of(levels)
+
+            @pl.when(part == PARTS - 1)
+            def _():
+                s_copy(h, role - 1).start()
+
+        over_others(action)
+
+    def mix_others(h):
+        def action(step, role, part):
+            for j in range(part_blocks):
+                b = part * part_blocks + j
                 span = pl.ds(pl.multiple_of(b * TILE, TILE), TILE)
-                osend[h, role - 1, span, :] = mixed.astype(jnp.bfloat16)
-                levels.append(level)
-            ssend[h, role - 1, part] = rows_of(levels)
-            for copy in o_copies(h, part, role - 1):
-                copy.start()
-            if h + 1 < heads:
-
-                @pl.when(is_mid & (step == others - 1))
-                def _():
-                    relay_on(h + 1)
-
-    def attend_own(h):
+                osend[h, role - 1, span, :] = mix(h, role, b, []).astype(jnp.bfloat16)
+            o_copy(h, part, role - 1).start()
+
+        over_others(action)
+
+    def weigh_own(h):
         @pl.loop(0, PARTS)
         def _(part):
             levels = []
             for j in range(part_blocks):
                 b = part * part_blocks + j
-                mixed, level = partial(
-                    h, 0, b, q_ref[b, :, head_columns(h)],
-                    [k_ref[b, :, head_columns(h)]], [v_ref[b, :, head_columns(h)]],
-                )
-                oself[pl.ds(pl.multiple_of(b * TILE, TILE), TILE), :] = mixed
-                levels.append(level)
+                query = q_ref[b, :, head_columns(h)]
+                levels.append(weigh(h, 0, b, query, [k_ref[b, :, head_columns(h)]]))
             sself[part] = rows_of(levels)
+
+    def mix_own(h):
+        @pl.loop(0, PARTS)
+        def _(part):
+            for j in range(part_blocks):
+                b = part * part_blocks + j
+                span = pl.ds(pl.multiple_of(b * TILE, TILE), TILE)
+                oself[span, :] = mix(h, 0, b, [v_ref[b, :, head_columns(h)]])
 
     def merge(h, part, slots):
         levels = [sself[part]] + [srecv[h, slot, part] for slot in range(slots)]
-        top = functools.reduce(jnp.maximum, levels)
-        shares = [jnp.exp2(level - top) for level in levels]
-        total = functools.reduce(jnp.add, shares)
-        spare = TILE - SUBLANES * len(shares)
+        tops = [level[:part_blocks] for level in levels]
+        denoms = [level[part_blocks:] for level in levels]
+        top = functools.reduce(jnp.maximum, tops)
+        shares = [jnp.exp2(one - top) for one in tops]
+        total = functools.reduce(jnp.add, [share * d for share, d in zip(shares, denoms)])
+        spare = TILE - part_blocks * len(shares)
         tall = jnp.concatenate(
             [share / total for share in shares] + [jnp.zeros((spare, TILE), F32)], axis=0
         ).T
@@ -580,13 +627,12 @@
             span = pl.ds((part * part_blocks + j) * TILE, TILE)
             value = oself[span, :] * tall[:, j : j + 1]
             for slot in range(slots):
-                column = SUBLANES * (slot + 1) + j
+                column = part_blocks * (slot + 1) + j
                 value = value + orecv[h, slot, span, :].astype(F32) * tall[:, column : column + 1]
             attn[h, me_p, span, :] = value.astype(jnp.bfloat16)
 
     def combine(h, part):
-        for copy in o_copies(h, part, 0):
-            copy.wait_recv()
+        o_copy(h, part, 0).wait_recv()
 
         @pl.when(is_mid)
         def _():
@@ -595,33 +641,49 @@
         @pl.when(is_end)
         def _():
             for slot in (1, 2):
-                for copy in o_copies(h, part, slot):
-                    copy.wait_recv()
+                o_copy(h, part, slot).wait_recv()
             merge(h, part, 3)
 
     def relay_on(h):
+        last = h == heads - 1
         for which in range(2):
             kv_copy(h, 0, which).wait_recv()
             kv_copy(h, 2, which).start()
-        if h + 1 < heads:
-            for which in range(2):
-                kv_copy(h + 1, 1, which).start()
+            if last and h > 0 and which == 0:
+                kv_copy(h, 1, 1).start()
+        if not last:
+            kv_copy(h + 1, 1, 0).start()
+            if h + 1 < heads - 1:
+                kv_copy(h + 1, 1, 1).start()
         q_copy(h, 1).wait_recv()
         q_copy(h, 2).start()
 
     def send_early(h):
-        q_copy(h, 0).start()
-
         @pl.when(is_end)
         def _():
             for which in range(2):
                 kv_copy(h, 0, which).start()
             q_copy(h, 1).start()
 
+    def open_column():
+        @pl.when(is_mid)
+        def _():
+            for which in range(2):
+                kv_copy(0, 1, which).start()
+
+        for h in range(early):
+            send_early(h)
+
+    early = min(EARLY, heads)
+    leads = lax.rem(me_p, 2) == 1
+
     def send_rows(h):
         over_peers(lambda target: w_copy(h, target, me_p).start())
 
-    pl.semaphore_wait(barrier, frames + peers - 2)
+    pl.semaphore_wait(barrier, peers + 2 + away)
+    for load in loads:
+        load.wait()
+
     c_copy(0).start()
 
     @pl.when(is_end)
@@ -629,17 +691,37 @@
         c_copy(1).start()
         c_copy(2).start()
 
-    @pl.when(is_mid)
+    @pl.when(leads)
     def _():
-        for which in range(2):
-            kv_copy(0, 1, which).start()
-
-    for h in range(min(EARLY, heads)):
-        send_early(h)
+        open_column()
+
+    for h in range(early):
+        q_copy(h, 0).start()
         send_rows(h)
-    count[0] = own_count_ref[...]
     fill_tables()
     own_block(0)
+
+    def first_sent(flow):
+        for which in range(2):
+            kv_copy(0, flow, which).wait_send()
+
+    @pl.when(leads & is_end)
+    def _():
+        first_sent(0)
+
+    @pl.when(leads & is_mid)
+    def _():
+        first_sent(1)
+
+    @pl.when(leads)
+    def _():
+        pl.semaphore_signal(turn_sem, inc=1, device_id=(me_f, twin), device_id_type=MESH)
+
+    @pl.when(jnp.logical_not(leads))
+    def _():
+        pl.semaphore_wait(turn_sem, 1)
+        open_column()
+
     c_copy(0).wait_recv()
 
     @pl.when(is_mid)
@@ -648,31 +730,114 @@
         c_copy(1).wait_recv()
         c_copy(2).wait_recv()
 
+    def drain_sends(h):
+        over_peers(lambda target: w_copy(h, target, me_p).wait_send())
+        q_copy(h, 0).wait_send()
+        started_here = jnp.logical_not(leads) if h == 0 else h >= 0
+
+        @pl.when(is_end & started_here)
+        def _():
+            for which in range(2):
+                kv_copy(h, 0, which).wait_send()
+
+        @pl.when(is_mid & started_here)
+        def _():
+            for which in range(2):
+                kv_copy(h, 1, which).wait_send()
+
+        @pl.when(is_end)
+        def _():
+            q_copy(h, 1).wait_send()
+
+        @pl.when(is_mid)
+        def _():
+            for which in range(2):
+                kv_copy(h, 2, which).wait_send()
+            q_copy(h, 2).wait_send()
+
+    def drain_partials(h):
+        @pl.loop(0, 1 + 2 * away)
+        def _(slot):
+            s_copy(h, slot).wait_send()
+            for part in range(PARTS):
+                o_copy(h, part, slot).wait_send()
+
+    def settle(h):
+        if h >= 0:
+            drain_sends(h)
+            drain_partials(h)
+            finish(h)
+        if h >= 1:
+            for part in range(PARTS):
+                drain_attn(h - 1, part)
+
     for h in range(heads):
         if h + EARLY < heads:
+            q_copy(h + EARLY, 0).start()
             send_early(h + EARLY)
         if h > 0:
             own_block(h)
+        last = h == heads - 1
+
+        def catch_up():
+            settle(h - 2)
+            if h > 0:
+                pass_on(h - 1)
+
+        if 0 < h < heads - 1:
+
+            @pl.when(is_mid)
+            def _():
+                relay_on(h + 1)
+
+        if last:
+            catch_up()
+            if h > 0:
+
+                @pl.when(jnp.logical_not(leads))
+                def _():
+                    finish(h - 1)
+
         q_copy(h, 0).wait_recv()
 
+        def arrived(which):
+            kv_copy(h, 1, which).wait_recv()
+            kv_copy(h, 2, which).wait_recv()
+
         @pl.when(is_mid)
         def _():
-            for which in range(2):
-                kv_copy(h, 1, which).wait_recv()
-                kv_copy(h, 2, which).wait_recv()
             q_copy(h, 2).wait_recv()
-
-        attend_others(h)
-        attend_own(h)
-        if h > 0:
-            finish(h - 1)
+            arrived(0)
+
+        weigh_others(h)
+        weigh_own(h)
+
+        @pl.when(is_mid)
+        def _():
+            arrived(1)
+
+        mix_others(h)
+        mix_own(h)
+        if not last:
+            if h == 0:
+
+                @pl.when(is_mid)
+                def _():
+                    relay_on(h + 1)
+
+            catch_up()
+        s_copy(h, 0).wait_recv()
+
+        @pl.when(is_end)
+        def _():
+            for slot in (1, 2):
+                s_copy(h, slot).wait_recv()
+
         for part in range(PARTS):
             combine(h, part)
             share(h, part)
         if h + EARLY < heads:
             send_rows(h + EARLY)
-    finish(heads - 1)
-
     c_copy(0).wait_send()
 
     @pl.when(is_end)
@@ -680,30 +845,23 @@
         c_copy(1).wait_send()
         c_copy(2).wait_send()
 
-    for h in range(heads):
-        over_peers(lambda target: w_copy(h, target, me_p).wait_send())
-        q_copy(h, 0).wait_send()
-
-        @pl.when(is_end)
-        def _():
-            for which in range(2):
-                kv_copy(h, 0, which).wait_send()
-            q_copy(h, 1).wait_send()
-
-        @pl.when(is_mid)
-        def _():
-            for which in range(2):
-                kv_copy(h, 1, which).wait_send()
-                kv_copy(h, 2, which).wait_send()
-            q_copy(h, 2).wait_send()
-
+    if heads > 1:
+
+        @pl.when(leads)
+        def _():
+            finish(heads - 2)
+
+        drain_sends(heads - 2)
+        drain_partials(heads - 2)
+    drain_sends(heads - 1)
+    pass_on(heads - 1)
+    finish(heads - 1)
+    drain_partials(heads - 1)
+    for h in range(max(0, heads - 3), heads):
         for part in range(PARTS):
             drain_attn(h, part)
-
-            @pl.loop(0, others)
-            def _(slot):
-                for copy in o_copies(h, part, slot):
-                    copy.wait_send()
+    for r in range(PARTS * part_rows // row_tile):
+        out_copy(r).wait()
 
 
 def column_shards(queries, keys, values, block_ids, counts, w_out):
@@ -715,12 +873,11 @@
     heads = width // DH
     features = w_out.shape[1] // peers
     smem = pl.BlockSpec(memory_space=pltpu.SMEM)
-    vmem = pl.BlockSpec(memory_space=pltpu.VMEM)
     tiles = (blocks, TILE, width)
     dma = pltpu.SemaphoreType.DMA
     bf16 = jnp.bfloat16
-    level_rows = (PARTS, SUBLANES, TILE)
-    scratch = [
+    level_rows = (PARTS, 2 * blocks // PARTS, TILE)
+    scratch = [pltpu.VMEM(tiles, bf16)] * 3 + [
         pltpu.VMEM((peers, width, features), bf16),
         pltpu.VMEM((heads, peers, tokens, DH), bf16),
         pltpu.VMEM((tokens, features), F32),
@@ -732,27 +889,30 @@
         pltpu.VMEM((heads, 3) + level_rows, F32),
         pltpu.VMEM((tokens, DH), F32),
         pltpu.VMEM(level_rows, F32),
+        pltpu.VMEM((4, blocks, TILE, (select + 1) * TILE), bf16),
+        pltpu.VMEM((tokens, features), bf16),
         pltpu.SMEM((4 * blocks * select,), jnp.int32),
         pltpu.SMEM((4 * blocks * select,), jnp.int32),
-        dma((heads, peers)), dma((heads, peers)), dma((heads, PARTS, peers, peers)),
-        dma((heads, PARTS, peers)), dma,
+        dma((heads, peers)), dma((heads, peers)), dma((heads, PARTS, peers)),
+        dma((heads, PARTS, peers)), dma, dma((3,)), pltpu.SemaphoreType.REGULAR,
+        dma((tokens // (2 * TILE),)),
         dma((3, heads, 2)), dma((3, heads, 2)), dma((3, heads)), dma((3, heads)),
         dma((3,)), dma((3,)),
-        dma((heads, PARTS, 3)), dma((heads, PARTS, 3)),
-        dma((heads, PARTS, 3)), dma((heads, PARTS, 3)),
-    ] + [pltpu.VMEM((2, 4 * blocks, TILE, DH), bf16)] * heads
+        dma((heads, PARTS, 3)), dma((heads, PARTS, 3)), dma((heads, 3)), dma((heads, 3)),
+    ] + [pltpu.VMEM((4 * blocks, TILE, DH), bf16)] * (2 * heads)
     dims = (frames, peers, blocks, select, heads)
+    hbm = pl.BlockSpec(memory_space=pltpu.HBM)
     return pl.pallas_call(
         functools.partial(column_kernel, dims),
         out_shape=jax.ShapeDtypeStruct((tokens, features), bf16),
-        in_specs=[smem, vmem, vmem, vmem, vmem, pl.BlockSpec(memory_space=pl.ANY)],
-        out_specs=vmem,
+        in_specs=[smem, smem, hbm, hbm, hbm, hbm],
+        out_specs=hbm,
         scratch_shapes=scratch,
         compiler_params=pltpu.CompilerParams(
             collective_id=0, has_side_effects=True, vmem_limit_bytes=VMEM_BYTES
         ),
     )(
-        block_ids.T, jnp.broadcast_to(counts[:, None], (blocks, TILE)),
+        block_ids.T, counts,
         queries.reshape(tiles), keys.reshape(tiles), values.reshape(tiles), w_out,
     )
 

time: 154 us -> 146 us (0.948)
  Pallas kernels: 148 us -> 143 us
    pallas_call x1, Pallas kernels: 148 us -> 143 us  [column_shards(): pl.pallas_call(functools.partial(column_kernel, dims), out_shape=jax.Shap...]
where the time goes in v2:
time: 146 us
  Pallas kernels  143 us (98%)
  local copies, waits for them, and re-layouts  3.4 us (2%)
    pallas_call x1, Pallas kernels, column_shards(): pl.pallas_call(functools.partial(column_kernel, dims), out_shape=jax.Shap...  143 us
    unnamed x1, local copies, waits for them, and re-layouts  3.4 us

profile of v2, /device:TPU:0, one launch (start us, length us, event | category | flops | bytes accessed | tf_op | source)
XLA Modules:
  0.0 145.9 jit_solution(18236263091781023471)
XLA Ops:
  0.0 142.5 %shard_map.64 = bf16[1024,1280]{1,0:T(8,128)(2,1)} custom-call(s32[4,64]{1,0:T(4,128)} %bitcast.7, s32[8]{0:T(128)} %own_count_ref.1, bf16[8,128,640]{2,1,0:T(8,128)(2,1)} %bitcast.4, bf16[8,128,640]{2,1,0:T(8,128)(2,1)} %bitcast.5, bf16[8,128,640]{2,1,0:T(8,128)(2,1)} %bitcast.6, bf16[640,5120]{1,0:T(8,128)(2,1)} %w_ref.1), custom_call_target="tpu_custom_call" | custom-call | tf_op jit(solution)/shard_map/pallas_call | solution.py:905
  142.5 3.4 %copy.8 = bf16[1024,1280]{1,0:T(8,128)(2,1)} copy(bf16[1024,1280]{1,0:T(8,128)(2,1)} %shard_map.64) | data formatting | bytes 5242880

commit v3 on v2

--- a/solution.py
+++ b/solution.py
@@ -379,14 +379,14 @@
             source = held.at[pl.ds(blocks, blocks)]
         return send(
             source, held.at[pl.ds((flow + 1) * blocks, blocks)],
-            kv_send.at[flow, h, which], kv_recv.at[flow, h, which],
+            kv_send.at[flow, which, int(h > 0)], kv_recv.at[flow, h, which],
             at(mid, x) if flow == 0 else at(across, x),
         )
 
     def q_copy(h, flow):
         source = q_ref.at[:, :, head_columns(h)] if flow < 2 else qall.at[h, 1]
         return send(
-            source, qall.at[h, flow], q_send.at[flow, h], q_recv.at[flow, h],
+            source, qall.at[h, flow], q_send.at[flow], q_recv.at[flow, h],
             at(mid, x) if flow == 1 else at(z, other),
         )
 
@@ -405,12 +405,12 @@
         span = pl.ds(part * part_rows, part_rows)
         return send(
             osend.at[h, slot, span], orecv.at[h, slot, span],
-            o_send.at[h, part, slot], o_recv.at[h, part, slot], partial_device(slot),
+            o_send.at[slot], o_recv.at[h, part, slot], partial_device(slot),
         )
 
     def s_copy(h, slot):
         return send(
-            ssend.at[h, slot], srecv.at[h, slot], s_send.at[h, slot], s_recv.at[h, slot],
+            ssend.at[h, slot], srecv.at[h, slot], s_send.at[slot], s_recv.at[h, slot],
             partial_device(slot),
         )
 
@@ -418,7 +418,7 @@
         span = pl.ds(h * DH, DH)
         return send(
             w_ref.at[span, columns_of(target)], rows.at[origin, span],
-            w_send.at[h, target], w_recv.at[h, origin], (me_f, target),
+            w_send.at[target], w_recv.at[h, origin], (me_f, target),
         )
 
     def a_copy(h, part, target, origin):
@@ -426,7 +426,7 @@
         to_twin = lax.rem(target + me_p, 2)
         lane_of = target + to_twin * (origin - me_p)
         return send(
-            held, held, a_send.at[h, part, lane_of], a_recv.at[h, part, origin],
+            held, held, a_send.at[lane_of], a_recv.at[h, part, origin],
             (me_f, target),
         )
 
@@ -467,11 +467,6 @@
         for part in range(PARTS):
             over_twins(lambda origin: a_copy(h, part, origin, origin).wait_recv())
             project(h, part)
-
-    def drain_attn(h, part):
-        over_alike(lambda target: a_copy(h, part, target, me_p).wait_send())
-        a_copy(h, part, twin, me_p).wait_send()
-        over_alike(lambda origin: a_copy(h, part, twin, origin).wait_send())
 
     row_tile = 2 * TILE
 
@@ -730,46 +725,53 @@
         c_copy(1).wait_recv()
         c_copy(2).wait_recv()
 
-    def drain_sends(h):
-        over_peers(lambda target: w_copy(h, target, me_p).wait_send())
-        q_copy(h, 0).wait_send()
-        started_here = jnp.logical_not(leads) if h == 0 else h >= 0
-
-        @pl.when(is_end & started_here)
-        def _():
+    def all_sent(source, semaphore):
+        pltpu.make_async_remote_copy(
+            src_ref=source, dst_ref=source, send_sem=semaphore, recv_sem=semaphore,
+            device_id=(me_f, twin), device_id_type=MESH,
+        ).wait_send()
+
+    def drain_early():
+        rest = pl.ds(DH, depth - DH)
+
+        def kv_sent(flow):
             for which in range(2):
-                kv_copy(h, 0, which).wait_send()
-
-        @pl.when(is_mid & started_here)
-        def _():
-            for which in range(2):
-                kv_copy(h, 1, which).wait_send()
+                if heads > 1:
+                    all_sent(k_ref.at[:, :, rest], kv_send.at[flow, which, 1])
+
+                @pl.when(jnp.logical_not(leads) | (flow == 2))
+                def _():
+                    all_sent(k_ref.at[:, :, pl.ds(0, DH)], kv_send.at[flow, which, 0])
+
+        c_copy(0).wait_send()
+        all_sent(q_ref, q_send.at[0])
+        over_peers(lambda target: all_sent(w_ref.at[:, columns_of(target)], w_send.at[target]))
 
         @pl.when(is_end)
         def _():
-            q_copy(h, 1).wait_send()
+            c_copy(1).wait_send()
+            c_copy(2).wait_send()
+            all_sent(q_ref, q_send.at[1])
+            kv_sent(0)
 
         @pl.when(is_mid)
         def _():
-            for which in range(2):
-                kv_copy(h, 2, which).wait_send()
-            q_copy(h, 2).wait_send()
-
-    def drain_partials(h):
+            all_sent(q_ref, q_send.at[2])
+            kv_sent(1)
+            kv_sent(2)
+
+    def drain_late():
         @pl.loop(0, 1 + 2 * away)
         def _(slot):
-            s_copy(h, slot).wait_send()
-            for part in range(PARTS):
-                o_copy(h, part, slot).wait_send()
+            all_sent(ssend.at[:, slot], s_send.at[slot])
+            all_sent(osend.at[:, slot], o_send.at[slot])
+
+        over_alike(lambda target: all_sent(attn.at[:, me_p], a_send.at[target]))
+        over_twins(lambda origin: all_sent(attn.at[:, me_p], a_send.at[origin]))
 
     def settle(h):
         if h >= 0:
-            drain_sends(h)
-            drain_partials(h)
             finish(h)
-        if h >= 1:
-            for part in range(PARTS):
-                drain_attn(h - 1, part)
 
     for h in range(heads):
         if h + EARLY < heads:
@@ -791,12 +793,10 @@
                 relay_on(h + 1)
 
         if last:
-            catch_up()
-            if h > 0:
-
-                @pl.when(jnp.logical_not(leads))
-                def _():
-                    finish(h - 1)
+
+            @pl.when(jnp.logical_not(leads))
+            def _():
+                settle(h - 2)
 
         q_copy(h, 0).wait_recv()
 
@@ -811,6 +811,8 @@
 
         weigh_others(h)
         weigh_own(h)
+        if last and h > 0:
+            pass_on(h - 1)
 
         @pl.when(is_mid)
         def _():
@@ -826,6 +828,12 @@
                     relay_on(h + 1)
 
             catch_up()
+        elif h > 0:
+
+            @pl.when(jnp.logical_not(leads))
+            def _():
+                finish(h - 1)
+
         s_copy(h, 0).wait_recv()
 
         @pl.when(is_end)
@@ -838,28 +846,15 @@
             share(h, part)
         if h + EARLY < heads:
             send_rows(h + EARLY)
-    c_copy(0).wait_send()
-
-    @pl.when(is_end)
+    @pl.when(leads)
     def _():
-        c_copy(1).wait_send()
-        c_copy(2).wait_send()
-
-    if heads > 1:
-
-        @pl.when(leads)
-        def _():
-            finish(heads - 2)
-
-        drain_sends(heads - 2)
-        drain_partials(heads - 2)
-    drain_sends(heads - 1)
+        settle(heads - 3)
+        settle(heads - 2)
+
+    drain_early()
     pass_on(heads - 1)
     finish(heads - 1)
-    drain_partials(heads - 1)
-    for h in range(max(0, heads - 3), heads):
-        for part in range(PARTS):
-            drain_attn(h, part)
+    drain_late()
     for r in range(PARTS * part_rows // row_tile):
         out_copy(r).wait()
 
@@ -893,12 +888,12 @@
         pltpu.VMEM((tokens, features), bf16),
         pltpu.SMEM((4 * blocks * select,), jnp.int32),
         pltpu.SMEM((4 * blocks * select,), jnp.int32),
-        dma((heads, peers)), dma((heads, peers)), dma((heads, PARTS, peers)),
+        dma((peers,)), dma((heads, peers)), dma((peers,)),
         dma((heads, PARTS, peers)), dma, dma((3,)), pltpu.SemaphoreType.REGULAR,
         dma((tokens // (2 * TILE),)),
-        dma((3, heads, 2)), dma((3, heads, 2)), dma((3, heads)), dma((3, heads)),
+        dma((3, 2, 2)), dma((3, heads, 2)), dma((3,)), dma((3, heads)),
         dma((3,)), dma((3,)),
-        dma((heads, PARTS, 3)), dma((heads, PARTS, 3)), dma((heads, 3)), dma((heads, 3)),
+        dma((3,)), dma((heads, PARTS, 3)), dma((3,)), dma((heads, 3)),
     ] + [pltpu.VMEM((4 * blocks, TILE, DH), bf16)] * (2 * heads)
     dims = (frames, peers, blocks, select, heads)
     hbm = pl.BlockSpec(memory_space=pltpu.HBM)

time: 146 us -> 142 us (0.973)
  Pallas kernels: 143 us -> 138 us
    pallas_call x1, Pallas kernels: 143 us -> 138 us  [column_shards(): pl.pallas_call(functools.partial(column_kernel, dims), out_shape=jax.Shap...]
where the time goes in v3:
time: 142 us
  Pallas kernels  138 us (97%)
  local copies, waits for them, and re-layouts  3.4 us (2%)
    pallas_call x1, Pallas kernels, column_shards(): pl.pallas_call(functools.partial(column_kernel, dims), out_shape=jax.Shap...  138 us
    unnamed x1, local copies, waits for them, and re-layouts  3.4 us

profile of v3, /device:TPU:0, one launch (start us, length us, event | category | flops | bytes accessed | tf_op | source)
XLA Modules:
  0.0 141.7 jit_solution(7835729638723993524)
XLA Ops:
  0.0 138.3 %shard_map.64 = bf16[1024,1280]{1,0:T(8,128)(2,1)} custom-call(s32[4,64]{1,0:T(4,128)} %bitcast.7, s32[8]{0:T(128)} %own_count_ref.1, bf16[8,128,640]{2,1,0:T(8,128)(2,1)} %bitcast.4, bf16[8,128,640]{2,1,0:T(8,128)(2,1)} %bitcast.5, bf16[8,128,640]{2,1,0:T(8,128)(2,1)} %bitcast.6, bf16[640,5120]{1,0:T(8,128)(2,1)} %w_ref.1), custom_call_target="tpu_custom_call" | custom-call | tf_op jit(solution)/shard_map/pallas_call | solution.py:900
  138.3 3.4 %copy.8 = bf16[1024,1280]{1,0:T(8,128)(2,1)} copy(bf16[1024,1280]{1,0:T(8,128)(2,1)} %shard_map.64) | data formatting | bytes 5242880

commit v4 on v3

--- a/solution.py
+++ b/solution.py
@@ -15,6 +15,8 @@
 PAIR = 2
 LINE = 4
 PARTS = 2
+LAST_PARTS = 4
+COPY_TILES = 8
 UNROLL = 2
 EARLY = 3
 LOG2E = math.log2(math.e)
@@ -326,12 +328,20 @@
     other = 1 - x
     depth = heads * DH
     features = rows.shape[2]
-    part_blocks = blocks // PARTS
-    part_rows = part_blocks * TILE
+    group_blocks = blocks // PARTS
     exponent = LOG2E / DH**0.5
 
     def at(zz, xx):
         return (zz * PAIR + xx, me_p)
+
+    def parts_of(h):
+        return LAST_PARTS if h == heads - 1 else PARTS
+
+    def rows_in(h):
+        return blocks // parts_of(h) * TILE
+
+    def rows_span(h, part):
+        return pl.ds(part * rows_in(h), rows_in(h))
 
     loads = [
         pltpu.make_async_copy(source, held, load_sem.at[i])
@@ -402,10 +412,10 @@
         return at(to_z, to_x)
 
     def o_copy(h, part, slot):
-        span = pl.ds(part * part_rows, part_rows)
+        span = rows_span(h, part)
         return send(
             osend.at[h, slot, span], orecv.at[h, slot, span],
-            o_send.at[slot], o_recv.at[h, part, slot], partial_device(slot),
+            o_send.at[slot], o_recv.at[h * PARTS + part, slot], partial_device(slot),
         )
 
     def s_copy(h, slot):
@@ -422,11 +432,11 @@
         )
 
     def a_copy(h, part, target, origin):
-        held = attn.at[h, origin, pl.ds(part * part_rows, part_rows)]
+        held = attn.at[h, origin, rows_span(h, part)]
         to_twin = lax.rem(target + me_p, 2)
         lane_of = target + to_twin * (origin - me_p)
         return send(
-            held, held, a_send.at[lane_of], a_recv.at[h, part, origin],
+            held, held, a_send.at[lane_of], a_recv.at[h * PARTS + part, origin],
             (me_f, target),
         )
 
@@ -451,22 +461,20 @@
         over_alike(lambda target: a_copy(h, part, target, me_p).start())
         a_copy(h, part, twin, me_p).start()
 
-    def pass_on(h):
-        for part in range(PARTS):
-
-            def relay(origin):
-                a_copy(h, part, origin, origin).wait_recv()
-                a_copy(h, part, twin, origin).start()
-
-            over_alike(relay)
-
-    def finish(h):
-        if h == 0:
-            own_rows.wait()
-        over_peers(lambda origin: w_copy(h, origin, origin).wait_recv())
-        for part in range(PARTS):
-            over_twins(lambda origin: a_copy(h, part, origin, origin).wait_recv())
-            project(h, part)
+    def pass_on(h, part):
+        def relay(origin):
+            a_copy(h, part, origin, origin).wait_recv()
+            a_copy(h, part, twin, origin).start()
+
+        over_alike(relay)
+
+    def finish(h, part):
+        if part == 0:
+            if h == 0:
+                own_rows.wait()
+            over_peers(lambda origin: w_copy(h, origin, origin).wait_recv())
+        over_twins(lambda origin: a_copy(h, part, origin, origin).wait_recv())
+        project(h, part)
 
     row_tile = 2 * TILE
 
@@ -475,7 +483,9 @@
         return pltpu.make_async_copy(finished.at[span], out_ref.at[span], out_sem.at[r])
 
     def project(h, part):
-        @pl.loop(part * part_rows // row_tile, (part + 1) * part_rows // row_tile)
+        tiles = rows_in(h) // row_tile
+
+        @pl.loop(part * tiles, (part + 1) * tiles)
         def _(r):
             span = pl.ds(pl.multiple_of(r * row_tile, row_tile), row_tile)
             left = jnp.concatenate([attn[h, p, span, :] for p in range(peers)], axis=1)
@@ -550,15 +560,15 @@
         tile = jnp.zeros((TILE, TILE), F32)
         for j, (top, denom) in enumerate(levels):
             tile = jnp.where(lane == j, top, tile)
-            tile = jnp.where(lane == part_blocks + j, denom, tile)
-        return tile.T[: 2 * part_blocks]
+            tile = jnp.where(lane == group_blocks + j, denom, tile)
+        return tile.T[: 2 * group_blocks]
 
     away = is_mid.astype(jnp.int32)
 
-    def over_others(action):
-        first = 2 * PARTS
-
-        @pl.loop(first * (1 - away), first + PARTS)
+    def over_others(parts, action):
+        first = 2 * parts
+
+        @pl.loop(first * (1 - away), first + parts)
         def _(step):
             late = step // first
             role = late + (1 - late) * (3 - step % 2)
@@ -568,8 +578,8 @@
     def weigh_others(h):
         def action(step, role, part):
             levels = []
-            for j in range(part_blocks):
-                b = part * part_blocks + j
+            for j in range(group_blocks):
+                b = part * group_blocks + j
                 levels.append(weigh(h, role, b, qall[h, role - 1, b], []))
             ssend[h, role - 1, part] = rows_of(levels)
 
@@ -577,9 +587,11 @@
             def _():
                 s_copy(h, role - 1).start()
 
-        over_others(action)
+        over_others(PARTS, action)
 
     def mix_others(h):
+        part_blocks = blocks // parts_of(h)
+
         def action(step, role, part):
             for j in range(part_blocks):
                 b = part * part_blocks + j
@@ -587,14 +599,14 @@
                 osend[h, role - 1, span, :] = mix(h, role, b, []).astype(jnp.bfloat16)
             o_copy(h, part, role - 1).start()
 
-        over_others(action)
+        over_others(parts_of(h), action)
 
     def weigh_own(h):
         @pl.loop(0, PARTS)
         def _(part):
             levels = []
-            for j in range(part_blocks):
-                b = part * part_blocks + j
+            for j in range(group_blocks):
+                b = part * group_blocks + j
                 query = q_ref[b, :, head_columns(h)]
                 levels.append(weigh(h, 0, b, query, [k_ref[b, :, head_columns(h)]]))
             sself[part] = rows_of(levels)
@@ -602,27 +614,30 @@
     def mix_own(h):
         @pl.loop(0, PARTS)
         def _(part):
-            for j in range(part_blocks):
-                b = part * part_blocks + j
+            for j in range(group_blocks):
+                b = part * group_blocks + j
                 span = pl.ds(pl.multiple_of(b * TILE, TILE), TILE)
                 oself[span, :] = mix(h, 0, b, [v_ref[b, :, head_columns(h)]])
 
     def merge(h, part, slots):
-        levels = [sself[part]] + [srecv[h, slot, part] for slot in range(slots)]
-        tops = [level[:part_blocks] for level in levels]
-        denoms = [level[part_blocks:] for level in levels]
+        part_blocks = blocks // parts_of(h)
+        group, first = divmod(part * part_blocks, group_blocks)
+        levels = [sself[group]] + [srecv[h, slot, group] for slot in range(slots)]
+        tops = [level[:group_blocks] for level in levels]
+        denoms = [level[group_blocks:] for level in levels]
         top = functools.reduce(jnp.maximum, tops)
         shares = [jnp.exp2(one - top) for one in tops]
         total = functools.reduce(jnp.add, [share * d for share, d in zip(shares, denoms)])
-        spare = TILE - part_blocks * len(shares)
+        spare = TILE - group_blocks * len(shares)
         tall = jnp.concatenate(
             [share / total for share in shares] + [jnp.zeros((spare, TILE), F32)], axis=0
         ).T
         for j in range(part_blocks):
             span = pl.ds((part * part_blocks + j) * TILE, TILE)
-            value = oself[span, :] * tall[:, j : j + 1]
+            column = first + j
+            value = oself[span, :] * tall[:, column : column + 1]
             for slot in range(slots):
-                column = part_blocks * (slot + 1) + j
+                column = group_blocks * (slot + 1) + first + j
                 value = value + orecv[h, slot, span, :].astype(F32) * tall[:, column : column + 1]
             attn[h, me_p, span, :] = value.astype(jnp.bfloat16)
 
@@ -771,7 +786,8 @@
 
     def settle(h):
         if h >= 0:
-            finish(h)
+            for part in range(parts_of(h)):
+                finish(h, part)
 
     for h in range(heads):
         if h + EARLY < heads:
@@ -784,7 +800,8 @@
         def catch_up():
             settle(h - 2)
             if h > 0:
-                pass_on(h - 1)
+                for part in range(parts_of(h - 1)):
+                    pass_on(h - 1, part)
 
         if 0 < h < heads - 1:
 
@@ -812,7 +829,8 @@
         weigh_others(h)
         weigh_own(h)
         if last and h > 0:
-            pass_on(h - 1)
+            for part in range(parts_of(h - 1)):
+                pass_on(h - 1, part)
 
         @pl.when(is_mid)
         def _():
@@ -832,7 +850,7 @@
 
             @pl.when(jnp.logical_not(leads))
             def _():
-                finish(h - 1)
+                settle(h - 1)
 
         s_copy(h, 0).wait_recv()
 
@@ -841,7 +859,7 @@
             for slot in (1, 2):
                 s_copy(h, slot).wait_recv()
 
-        for part in range(PARTS):
+        for part in range(parts_of(h)):
             combine(h, part)
             share(h, part)
         if h + EARLY < heads:
@@ -852,11 +870,50 @@
         settle(heads - 2)
 
     drain_early()
-    pass_on(heads - 1)
-    finish(heads - 1)
+    for part in range(parts_of(heads - 1)):
+        pass_on(heads - 1, part)
+        if part > 0:
+            finish(heads - 1, part - 1)
+    finish(heads - 1, parts_of(heads - 1) - 1)
     drain_late()
-    for r in range(PARTS * part_rows // row_tile):
+    for r in range(blocks * TILE // row_tile):
         out_copy(r).wait()
+
+
+def place_result(result):
+    tokens, features = result.shape
+    rows = tokens // COPY_TILES
+
+    def kernel(source, target, held, read_sem, write_sem):
+        spans = [pl.ds(i * rows, rows) for i in range(COPY_TILES)]
+        reads = [
+            pltpu.make_async_copy(source.at[span], held.at[span], read_sem.at[i])
+            for i, span in enumerate(spans)
+        ]
+        writes = [
+            pltpu.make_async_copy(held.at[span], target.at[span], write_sem.at[i])
+            for i, span in enumerate(spans)
+        ]
+        for read in reads:
+            read.start()
+        for read, write in zip(reads, writes):
+            read.wait()
+            write.start()
+        for write in writes:
+            write.wait()
+
+    hbm = pl.BlockSpec(memory_space=pltpu.HBM)
+    return pl.pallas_call(
+        kernel,
+        out_shape=jax.ShapeDtypeStruct(result.shape, result.dtype),
+        in_specs=[hbm],
+        out_specs=hbm,
+        scratch_shapes=[
+            pltpu.VMEM(result.shape, result.dtype),
+            pltpu.SemaphoreType.DMA((COPY_TILES,)),
+            pltpu.SemaphoreType.DMA((COPY_TILES,)),
+        ],
+    )(result)
 
 
 def column_shards(queries, keys, values, block_ids, counts, w_out):
@@ -871,6 +928,7 @@
     tiles = (blocks, TILE, width)
     dma = pltpu.SemaphoreType.DMA
     bf16 = jnp.bfloat16
+    pieces = (heads - 1) * PARTS + LAST_PARTS
     level_rows = (PARTS, 2 * blocks // PARTS, TILE)
     scratch = [pltpu.VMEM(tiles, bf16)] * 3 + [
         pltpu.VMEM((peers, width, features), bf16),
@@ -889,15 +947,15 @@
         pltpu.SMEM((4 * blocks * select,), jnp.int32),
         pltpu.SMEM((4 * blocks * select,), jnp.int32),
         dma((peers,)), dma((heads, peers)), dma((peers,)),
-        dma((heads, PARTS, peers)), dma, dma((3,)), pltpu.SemaphoreType.REGULAR,
+        dma((pieces, peers)), dma, dma((3,)), pltpu.SemaphoreType.REGULAR,
         dma((tokens // (2 * TILE),)),
         dma((3, 2, 2)), dma((3, heads, 2)), dma((3,)), dma((3, heads)),
         dma((3,)), dma((3,)),
-        dma((3,)), dma((heads, PARTS, 3)), dma((3,)), dma((heads, 3)),
+        dma((3,)), dma((pieces, 3)), dma((3,)), dma((heads, 3)),
     ] + [pltpu.VMEM((4 * blocks, TILE, DH), bf16)] * (2 * heads)
     dims = (frames, peers, blocks, select, heads)
     hbm = pl.BlockSpec(memory_space=pltpu.HBM)
-    return pl.pallas_call(
+    result = pl.pallas_call(
         functools.partial(column_kernel, dims),
         out_shape=jax.ShapeDtypeStruct((tokens, features), bf16),
         in_specs=[smem, smem, hbm, hbm, hbm, hbm],
@@ -910,6 +968,7 @@
         block_ids.T, counts,
         queries.reshape(tiles), keys.reshape(tiles), values.reshape(tiles), w_out,
     )
+    return place_result(result)
 
 
 def solution(mesh):

time: 142 us -> 140 us (0.986)
  local copies, waits for them, and re-layouts: 3.4 us -> 0 us
    unnamed x1 -> x0, local copies, waits for them, and re-layouts: 3.4 us -> none
    pallas_call x0 -> x1, Pallas kernels: none -> 2.59 us  [place_result(): pl.pallas_call(kernel, out_shape=jax.ShapeDtypeStruct(result.shape, resul...]
    pallas_call x1, Pallas kernels: 138 us -> 137 us  [column_shards(): pl.pallas_call(functools.partial(column_kernel, dims), out_shape=jax.Shap...]
where the time goes in v4:
time: 140 us; the launch traced here: 139 us
  Pallas kernels  139 us (99%)
    pallas_call x1, Pallas kernels, column_shards(): pl.pallas_call(functools.partial(column_kernel, dims), out_shape=jax.Shap...  137 us

profile of v4, /device:TPU:0, one launch (start us, length us, event | category | flops | bytes accessed | tf_op | source)
XLA Modules:
  0.0 139.3 jit_solution(13203199578521510203)
XLA Ops:
  0.0 136.6 %shard_map.64.source = bf16[1024,1280]{1,0:T(8,128)(2,1)} custom-call(s32[4,64]{1,0:T(4,128)} %bitcast.7, s32[8]{0:T(128)} %own_count_ref.1, bf16[8,128,640]{2,1,0:T(8,128)(2,1)} %bitcast.4, bf16[8,128,640]{2,1,0:T(8,128)(2,1)} %bitcast.5, bf16[8,128,640]{2,1,0:T(8,128)(2,1)} %bitcast.6, bf16[640,5120]{1,0:T(8,128)(2,1)} %w_ref.1), custom_call_target="tpu_custom_call" | custom-call | tf_op jit(solution)/shard_map/pallas_call | solution.py:958
  136.6 2.6 %shard_map.65 = bf16[1024,1280]{1,0:T(8,128)(2,1)} custom-call(bf16[1024,1280]{1,0:T(8,128)(2,1)} %shard_map.64.source), custom_call_target="tpu_custom_call" | custom-call | tf_op jit(solution)/shard_map/pallas_call | solution.py:906

commit v5 on v4

--- a/solution.py
+++ b/solution.py
@@ -457,9 +457,15 @@
         def _(step):
             action(lax.rem(twin + 2 * step, peers))
 
+    def direct(h, part):
+        return h == heads - 1 and part >= parts_of(h) // 2
+
     def share(h, part):
         over_alike(lambda target: a_copy(h, part, target, me_p).start())
-        a_copy(h, part, twin, me_p).start()
+        if direct(h, part):
+            over_twins(lambda target: a_copy(h, part, target, me_p).start())
+        else:
+            a_copy(h, part, twin, me_p).start()
 
     def pass_on(h, part):
         def relay(origin):
@@ -473,6 +479,8 @@
             if h == 0:
                 own_rows.wait()
             over_peers(lambda origin: w_copy(h, origin, origin).wait_recv())
+        if direct(h, part):
+            over_alike(lambda origin: a_copy(h, part, origin, origin).wait_recv())
         over_twins(lambda origin: a_copy(h, part, origin, origin).wait_recv())
         project(h, part)
 
@@ -871,10 +879,10 @@
 
     drain_early()
     for part in range(parts_of(heads - 1)):
-        pass_on(heads - 1, part)
-        if part > 0:
-            finish(heads - 1, part - 1)
-    finish(heads - 1, parts_of(heads - 1) - 1)
+        if not direct(heads - 1, part):
+            pass_on(heads - 1, part)
+    for part in range(parts_of(heads - 1)):
+        finish(heads - 1, part)
     drain_late()
     for r in range(blocks * TILE // row_tile):
         out_copy(r).wait()

time: 140 us -> 139 us (level)
  no operation moved by 1% of the time
where the time goes in v5:
time: 139 us
  Pallas kernels  139 us (100%)
    pallas_call x1, Pallas kernels, column_shards(): pl.pallas_call(functools.partial(column_kernel, dims), out_shape=jax.Shap...  136 us

profile of v5, /device:TPU:0, one launch (start us, length us, event | category | flops | bytes accessed | tf_op | source)
XLA Modules:
  0.0 138.7 jit_solution(12676426565668055381)
XLA Ops:
  0.0 136.0 %shard_map.64.source = bf16[1024,1280]{1,0:T(8,128)(2,1)} custom-call(s32[4,64]{1,0:T(4,128)} %bitcast.7, s32[8]{0:T(128)} %own_count_ref.1, bf16[8,128,640]{2,1,0:T(8,128)(2,1)} %bitcast.4, bf16[8,128,640]{2,1,0:T(8,128)(2,1)} %bitcast.5, bf16[8,128,640]{2,1,0:T(8,128)(2,1)} %bitcast.6, bf16[640,5120]{1,0:T(8,128)(2,1)} %w_ref.1), custom_call_target="tpu_custom_call" | custom-call | tf_op jit(solution)/shard_map/pallas_call | solution.py:966
  136.0 2.6 %shard_map.65 = bf16[1024,1280]{1,0:T(8,128)(2,1)} custom-call(bf16[1024,1280]{1,0:T(8,128)(2,1)} %shard_map.64.source), custom_call_target="tpu_custom_call" | custom-call | tf_op jit(solution)/shard_map/pallas_call | solution.py:914

commit v6 on v5

--- a/solution.py
+++ b/solution.py
@@ -856,7 +856,7 @@
             catch_up()
         elif h > 0:
 
-            @pl.when(jnp.logical_not(leads))
+            @pl.when(jnp.logical_not(leads) & is_end)
             def _():
                 settle(h - 1)
 
@@ -870,6 +870,12 @@
         for part in range(parts_of(h)):
             combine(h, part)
             share(h, part)
+        if last and h > 0:
+
+            @pl.when(jnp.logical_not(leads) & is_mid)
+            def _():
+                settle(h - 1)
+
         if h + EARLY < heads:
             send_rows(h + EARLY)
     @pl.when(leads)

time: 139 us -> 139 us (level)
  no operation moved by 1% of the time
where the time goes in v6:
time: 139 us
  Pallas kernels  139 us (100%)
    pallas_call x1, Pallas kernels, column_shards(): pl.pallas_call(functools.partial(column_kernel, dims), out_shape=jax.Shap...  136 us

profile of v6, /device:TPU:0, one launch (start us, length us, event | category | flops | bytes accessed | tf_op | source)
XLA Modules:
  0.0 138.7 jit_solution(12352430805018748661)
XLA Ops:
  0.0 136.0 %shard_map.64.source = bf16[1024,1280]{1,0:T(8,128)(2,1)} custom-call(s32[4,64]{1,0:T(4,128)} %bitcast.7, s32[8]{0:T(128)} %own_count_ref.1, bf16[8,128,640]{2,1,0:T(8,128)(2,1)} %bitcast.4, bf16[8,128,640]{2,1,0:T(8,128)(2,1)} %bitcast.5, bf16[8,128,640]{2,1,0:T(8,128)(2,1)} %bitcast.6, bf16[640,5120]{1,0:T(8,128)(2,1)} %w_ref.1), custom_call_target="tpu_custom_call" | custom-call | tf_op jit(solution)/shard_map/pallas_call | solution.py:972
  136.0 2.6 %shard_map.65 = bf16[1024,1280]{1,0:T(8,128)(2,1)} custom-call(bf16[1024,1280]{1,0:T(8,128)(2,1)} %shard_map.64.source), custom_call_target="tpu_custom_call" | custom-call | tf_op jit(solution)/shard_map/pallas_call | solution.py:920
